TPU v7x, 256 devices: a 4x2x16 block of a 4x16x16 slice. The times are simulated.
256 devices in a mesh: groups: 2 (over y), dom: 32 (over z, core), shot: 4 (over x).
Axes of the slice: x: 4, y: 2, z: 16, core: 2. Of those that a mesh axis runs over, the one named last changes fastest.
The devices are a block of a 4x16x16 slice.
Arguments:
- courant_sq: float32 [1024, 128, 128], P(('groups', 'dom')), parts along dimension 0, may hold values from 0.05 to 0.19
- adjoint_init: float32 [8, 2, 512, 128, 128], P(('groups', 'shot'), None, 'dom'), parts along dimension 0, may hold values from -6 to 6
- forward_saved: bfloat16 [8, 6, 512, 128, 128], P(('groups', 'shot'), None, 'dom'), parts along dimension 0, may hold values from -4 to 4
- residual_traces: float32 [8, 4, 1024], P(('groups', 'shot')), parts along dimension 0, may hold values from -6 to 6
- receivers: int32 [8, 1024, 3], P(('groups', 'shot')), parts along dimension 0, may hold values from 0 to 511, as said below
- sources: int32 [8, 3], P(('groups', 'shot')), parts along dimension 0, may hold values from 0 to 511, as said below
Outputs:
- gradient: float32 [1024, 128, 128], P(('groups', 'dom'), 'shot'), parts along dimension 0
- adjoint_final: float32 [8, 2, 512, 128, 128], P(('groups', 'shot'), None, 'dom'), parts along dimension 0
There are 2 independent parts, one for each index of `groups`. A program takes and returns all parts, laid end to end along the dimension named above; each array names one. Nothing has to cross between parts.
Inputs may be any that keep to these rules, and one draw needn't show every extreme that they name: Each row holds the depth index (below 512), the first horizontal index (below 128) and the second (below 128) of a cell; receivers may share cells. `sources`: each row holds the depth index (below 512), the first horizontal index (below 128) and the second (below 128) of a cell.
All inputs are finite; a program needn't handle non-finite values.
Results may differ from a plain program's by a relative error of at most 0.0003.
Values sent between devices are 32-bit elements; how exact they have to be, the bound alone decides.
A program may use at most 64 MiB of HBM per device.

v0:
```python
import jax
import jax.numpy as jnp
from jax import lax
from jax.sharding import PartitionSpec as P

ITERS = 4
RADIUS = 6


STENCIL_WEIGHTS = (-205.0 / 72.0, 8.0 / 5.0, -1.0 / 5.0, 8.0 / 315.0, -1.0 / 560.0)


def padded_2(array, sides, width):
    for axis, dim in sides:
        size, length = (lax.axis_size(axis), array.shape[dim])
        up = [(i, (i + 1) % size) for i in range(size - 1)]
        down = [(j, i) for i, j in up]
        last = lax.slice_in_dim(array, length - width, length, axis=dim)
        initial = lax.slice_in_dim(array, 0, width, axis=dim)
        before = lax.ppermute(last, axis, up)
        after = lax.ppermute(initial, axis, down)
        array = jnp.concatenate([before, array, after], axis=dim)
    return array


def split_up(array, dim, size):
    before, after = (array.shape[:dim], array.shape[dim + 1 :])
    return jnp.moveaxis(array.reshape(*before, size, -1, *after), dim, 0)


def sum_at_owner(array, axis, dim):
    size = lax.axis_size(axis)
    pieces = lax.all_to_all(split_up(array, dim, size), axis, 0, 0, tiled=True)
    return jnp.sum(pieces, axis=0)


def stencil(level_now):
    row_count = level_now.shape[0] - 8
    size_x = level_now.shape[1]
    size_y = level_now.shape[2]
    center = level_now[4 : 4 + row_count]
    padded = jnp.pad(center, ((0, 0), (4, 4), (4, 4)))
    summed = 3.0 * STENCIL_WEIGHTS[0] * center
    for offset in range(1, 5):
        beside_all = (
            level_now[4 + offset : 4 + offset + row_count]
            + level_now[4 - offset : 4 - offset + row_count]
        )
        beside_all = beside_all + padded[:, 4 + offset : 4 + offset + size_x, 4 : 4 + size_y]
        beside_all = beside_all + padded[:, 4 - offset : 4 - offset + size_x, 4 : 4 + size_y]
        beside_all = beside_all + padded[:, 4 : 4 + size_x, 4 + offset : 4 + offset + size_y]
        beside_all = beside_all + padded[:, 4 : 4 + size_x, 4 - offset : 4 - offset + size_y]
        summed = summed + STENCIL_WEIGHTS[offset] * beside_all
    return summed


def source_taper(source, depth_first, size_z, size_x, size_y):
    depth_gap = jnp.arange(size_z, dtype=jnp.int32) + depth_first - source[0]
    across_gap = jnp.arange(size_x, dtype=jnp.int32) - source[1]
    along_gap = jnp.arange(size_y, dtype=jnp.int32) - source[2]
    distance = (
        (depth_gap * depth_gap)[:, None, None]
        + (across_gap * across_gap)[None, :, None]
        + (along_gap * along_gap)[None, None, :]
    )
    return 1.0 - jnp.exp(-distance.astype(jnp.float32) / float(RADIUS * RADIUS))


def advance(
    level_later,
    level_now,
    courant_ext,
    first_row,
    section_top,
    forward_saved,
    residual_traces,
    receivers,
    summed,
):
    slab_rows = forward_saved.shape[2]
    row_count = level_now.shape[0] - 8
    margin_out = (row_count - slab_rows) // 2
    level_next = (
        2.0 * level_now[4 : 4 + row_count]
        - level_later[4 : 4 + row_count]
        + courant_ext * stencil(level_now)
    )
    top_row = first_row - margin_out
    local_rows = receivers[0, :, 0] - top_row
    inside = (local_rows >= 0) & (local_rows < row_count)
    amounts = jnp.where(inside, residual_traces[0, section_top], 0.0)
    level_next = level_next.at[
        jnp.clip(local_rows, 0, row_count - 1), receivers[0, :, 1], receivers[0, :, 2]
    ].add(amounts)
    forward_accel = (
        forward_saved[0, section_top + 2].astype(jnp.float32)
        - 2.0 * forward_saved[0, section_top + 1].astype(jnp.float32)
        + forward_saved[0, section_top].astype(jnp.float32)
    )
    summed = summed + level_next * forward_accel
    level_later = level_now[4 : 4 + row_count]
    return (level_later, level_next, summed)


def per_device(courant_sq, adjoint_init, forward_saved, residual_traces, receivers, sources):
    slab_rows, size_x, size_y = courant_sq.shape
    first_row = lax.axis_index("dom") * slab_rows
    level_later = adjoint_init[0, 0]
    level_now = adjoint_init[0, 1]
    summed = jnp.zeros((slab_rows, size_x, size_y), jnp.float32)
    for block_index in range(ITERS):
        padded_now = padded_2(level_now, (("dom", 0),), 4)
        padded_later = jnp.pad(level_later, ((4, 4), (0, 0), (0, 0)))
        level_later, level_now, summed = advance(
            padded_later,
            padded_now,
            courant_sq,
            first_row,
            ITERS - 1 - block_index,
            forward_saved,
            residual_traces,
            receivers,
            summed,
        )
    tapered = source_taper(sources[0], first_row, slab_rows, size_x, size_y) * summed
    gradient = sum_at_owner(tapered, "shot", 1)
    return (gradient, jnp.stack([level_later, level_now])[None])


def solution(mesh):
    placed = (
        P(("groups", "dom"), None, None),
        P(("groups", "shot"), None, "dom", None, None),
        P(("groups", "shot"), None, "dom", None, None),
        P(("groups", "shot"), None, None),
        P(("groups", "shot"), None, None),
        P(("groups", "shot"), None),
    )
    return jax.shard_map(
        per_device,
        mesh=mesh,
        in_specs=placed,
        out_specs=(
            P(("groups", "dom"), "shot", None),
            P(("groups", "shot"), None, "dom", None, None),
        ),
        check_vma=False,
    )
```

profile of v0, /device:TPU:33, one launch (start us, length us, event | category | flops | bytes accessed | tf_op | source)
XLA Modules:
  0.0 124.9 jit_solution(12350893313021248308)
XLA Ops:
  0.6 1.1 slice_bitcast_fusion.2
  1.7 0.0 copy-start.1
  1.7 5.9 %collective-permute-start.1 = (f32[4,128,128]{2,1,0:T(8,128)S(1)}, f32[4,128,128]{2,1,0:T(8,128)S(1)}, u32[]{:S(2)}, u32[]{:S(2)}) collective-permute-start(f32[4,128,128]{2,1,0:T(8,128)S(1)} %get-tuple-element.3), channel_id=1, source_target_pairs={{0,4},{4,8},{8,12},{12,16},{16,20},{20,24},{24,28},{28,32},{32,36}... | collective-permute-start | bytes 786440 | tf_op jit(solution)/shard_map/ppermute | solution.py:20
  7.6 17.9 %collective-permute-start = (f32[4,128,128]{2,1,0:T(8,128)S(1)}, f32[4,128,128]{2,1,0:T(8,128)}, u32[]{:S(2)}, u32[]{:S(2)}) collective-permute-start(f32[4,128,128]{2,1,0:T(8,128)S(1)} %get-tuple-element.2), channel_id=1, source_target_pairs={{4,0},{8,4},{12,8},{16,12},{20,16},{24,20},{28,24},{32,28},{36,32}... | collective-permute-start | bytes 786440 | tf_op jit(solution)/shard_map/ppermute | solution.py:21
  25.5 0.7 compare_select_fusion.2
  26.3 0.7 and_reduce_fusion.1
  27.0 0.7 and_reduce_fusion
  27.7 0.7 multiply_reduce_fusion
  28.5 0.9 fusion.157
  29.4 1.3 %slice_bitcast_fusion = f32[16,128,128]{2,1,0:T(8,128)S(1)} fusion(f32[1,2,16,128,128]{4,3,2,1,0:T(8,128)} %param.7), kind=kLoop, calls=%fused_computation.290 | loop fusion | bytes 2097152 | tf_op jit(solution)/shard_map/squeeze | solution.py:109
  30.7 0.0 collective-permute-done.1
  30.7 0.0 collective-permute-done
  30.7 0.0 copy-done.1
  30.7 4.6 %fusion.105 = f32[16,128,128]{2,1,0:T(8,128)S(1)} fusion(f32[16,128,128]{2,1,0:T(8,128)S(1)} %copy-done.1, f32[16,128,128]{2,1,0:T(8,128)S(1)} %slice_bitcast_fusion, f32[4,128,128]{2,1,0:T(8,128)S(1)} %collective-permute-done.1, f32[4,128,128]{2,1,0:T(8,128)} %collective-permute-done, f32[1,2,16,128,128]{4,3,2,1,0:T(8,128)} %param.7), kind=kLoop, calls=%fused_computation.232 | loop fusion | flops 10747904 | bytes 4718592 | tf_op jit(solution)/shard_map/add | solution.py:84
  35.4 6.5 %scatter_fusion = f32[262144]{0:T(1024)S(1)} fusion(f32[262144]{0:T(1024)S(1)} %bitcast.64, s32[1024]{0:T(1024)S(1)} %broadcast_select_fusion, f32[1024]{0:T(1024)S(1)} %get-tuple-element.20), kind=kCustom, calls=%fused_computation | custom fusion | flops 1024 | bytes 16384
  41.9 2.0 %collective-permute-start.3 = (f32[4,128,128]{2,1,0:T(8,128)S(1)}, f32[4,128,128]{2,1,0:T(8,128)S(1)}, u32[]{:S(2)}, u32[]{:S(2)}) collective-permute-start(f32[4,128,128]{2,1,0:T(8,128)S(1)} %bitcast.85), channel_id=1, source_target_pairs={{0,4},{4,8},{8,12},{12,16},{16,20},{20,24},{24,28},{28,32},{32,36}... | collective-permute-start | bytes 786440 | tf_op jit(solution)/shard_map/ppermute | solution.py:20
  43.8 2.4 %collective-permute-start.2 = (f32[4,128,128]{2,1,0:T(8,128)S(1)}, f32[4,128,128]{2,1,0:T(8,128)S(1)}, u32[]{:S(2)}, u32[]{:S(2)}) collective-permute-start(f32[4,128,128]{2,1,0:T(8,128)S(1)} %bitcast.84), channel_id=1, source_target_pairs={{4,0},{8,4},{12,8},{16,12},{20,16},{24,20},{28,24},{32,28},{36,32}... | collective-permute-start | bytes 786440 | tf_op jit(solution)/shard_map/ppermute | solution.py:21
  46.3 0.8 collective-permute-done.3
  47.1 4.4 %collective-permute-done.2 = f32[4,128,128]{2,1,0:T(8,128)S(1)} collective-permute-done((f32[4,128,128]{2,1,0:T(8,128)S(1)}, f32[4,128,128]{2,1,0:T(8,128)S(1)}, u32[]{:S(2)}, u32[]{:S(2)}) %collective-permute-start.2) | collective-permute-done | bytes 262176 | tf_op jit(solution)/shard_map/ppermute | solution.py:21
  51.6 4.7 %fusion.75 = f32[16,128,128]{2,1,0:T(8,128)S(1)} fusion(f32[16,128,128]{2,1,0:T(8,128)S(1)} %copy-done.1, f32[16,128,128]{2,1,0:T(8,128)S(1)} %bitcast.65, f32[4,128,128]{2,1,0:T(8,128)S(1)} %collective-permute-done.3, f32[4,128,128]{2,1,0:T(8,128)S(1)} %collective-permute-done.2, f32[1,2,16,128,128]{4,3,2,1,0:T(8,128)} %param.7), kind=kLoop, calls=%fused_computation.202 | loop fusion | flops 10747904 | bytes 4718592 | tf_op jit(solution)/shard_map/add | solution.py:84
  56.3 0.0 copy-start.4
  56.3 6.5 %scatter_fusion.1 = f32[262144]{0:T(1024)S(1)} fusion(f32[262144]{0:T(1024)S(1)} %bitcast.68, s32[1024]{0:T(1024)S(1)} %broadcast_select_fusion, f32[1024]{0:T(1024)S(1)} %get-tuple-element.19), kind=kCustom, calls=%fused_computation.1 | custom fusion | flops 1024 | bytes 16384
  62.7 0.0 copy-start.2
  62.8 2.1 %collective-permute-start.5 = (f32[4,128,128]{2,1,0:T(8,128)S(1)}, f32[4,128,128]{2,1,0:T(8,128)S(1)}, u32[]{:S(2)}, u32[]{:S(2)}) collective-permute-start(f32[4,128,128]{2,1,0:T(8,128)S(1)} %bitcast.82), channel_id=1, source_target_pairs={{0,4},{4,8},{8,12},{12,16},{16,20},{20,24},{24,28},{28,32},{32,36}... | collective-permute-start | bytes 786440 | tf_op jit(solution)/shard_map/ppermute | solution.py:20
  64.9 2.4 %collective-permute-start.4 = (f32[4,128,128]{2,1,0:T(8,128)S(1)}, f32[4,128,128]{2,1,0:T(8,128)S(1)}, u32[]{:S(2)}, u32[]{:S(2)}) collective-permute-start(f32[4,128,128]{2,1,0:T(8,128)S(1)} %bitcast.80), channel_id=1, source_target_pairs={{4,0},{8,4},{12,8},{16,12},{20,16},{24,20},{28,24},{32,28},{36,32}... | collective-permute-start | bytes 786440 | tf_op jit(solution)/shard_map/ppermute | solution.py:21
  67.3 0.0 copy-done.4
  67.4 0.7 fusion.158
  68.0 0.6 subtract_multiply_fusion
  68.7 0.7 subtract_multiply_fusion.1
  69.4 0.0 collective-permute-done.5
  69.4 3.2 %collective-permute-done.4 = f32[4,128,128]{2,1,0:T(8,128)S(1)} collective-permute-done((f32[4,128,128]{2,1,0:T(8,128)S(1)}, f32[4,128,128]{2,1,0:T(8,128)S(1)}, u32[]{:S(2)}, u32[]{:S(2)}) %collective-permute-start.4) | collective-permute-done | bytes 262176 | tf_op jit(solution)/shard_map/ppermute | solution.py:21
  72.6 3.6 %fusion.45 = f32[16,128,128]{2,1,0:T(8,128)S(1)} fusion(f32[16,128,128]{2,1,0:T(8,128)S(1)} %copy-done.2, f32[16,128,128]{2,1,0:T(8,128)S(1)} %bitcast.69, f32[4,128,128]{2,1,0:T(8,128)S(1)} %collective-permute-done.5, f32[4,128,128]{2,1,0:T(8,128)S(1)} %collective-permute-done.4, f32[16,128,128]{2,1,0:T(8,128)S(1)} %bitcast.66), kind=kLoop, calls=%fused_computation.172 | loop fusion | flops 10747904 | bytes 4718592 | tf_op jit(solution)/shard_map/add | solution.py:84
  76.3 6.5 %scatter_fusion.2 = f32[262144]{0:T(1024)S(1)} fusion(f32[262144]{0:T(1024)S(1)} %bitcast.72, s32[1024]{0:T(1024)S(1)} %broadcast_select_fusion, f32[1024]{0:T(1024)S(1)} %get-tuple-element.18), kind=kCustom, calls=%fused_computation.2 | custom fusion | flops 1024 | bytes 16384
  82.7 0.0 copy-start.3
  82.8 2.1 %collective-permute-start.7 = (f32[4,128,128]{2,1,0:T(8,128)S(1)}, f32[4,128,128]{2,1,0:T(8,128)S(1)}, u32[]{:S(2)}, u32[]{:S(2)}) collective-permute-start(f32[4,128,128]{2,1,0:T(8,128)S(1)} %bitcast.83), channel_id=1, source_target_pairs={{0,4},{4,8},{8,12},{12,16},{16,20},{20,24},{24,28},{28,32},{32,36}... | collective-permute-start | bytes 786440 | tf_op jit(solution)/shard_map/ppermute | solution.py:20
  84.9 2.6 %collective-permute-start.6 = (f32[4,128,128]{2,1,0:T(8,128)S(1)}, f32[4,128,128]{2,1,0:T(8,128)S(1)}, u32[]{:S(2)}, u32[]{:S(2)}) collective-permute-start(f32[4,128,128]{2,1,0:T(8,128)S(1)} %bitcast.81), channel_id=1, source_target_pairs={{4,0},{8,4},{12,8},{16,12},{20,16},{24,20},{28,24},{32,28},{36,32}... | collective-permute-start | bytes 786440 | tf_op jit(solution)/shard_map/ppermute | solution.py:21
  87.5 0.7 subtract_multiply_fusion.2
  88.2 0.1 broadcast_add_fusion
  88.2 0.0 collective-permute-done.7
  88.2 4.4 %collective-permute-done.6 = f32[4,128,128]{2,1,0:T(8,128)S(1)} collective-permute-done((f32[4,128,128]{2,1,0:T(8,128)S(1)}, f32[4,128,128]{2,1,0:T(8,128)S(1)}, u32[]{:S(2)}, u32[]{:S(2)}) %collective-permute-start.6) | collective-permute-done | bytes 262176 | tf_op jit(solution)/shard_map/ppermute | solution.py:21
  92.6 4.4 %fusion.15 = f32[16,128,128]{2,1,0:T(8,128)} fusion(f32[16,128,128]{2,1,0:T(8,128)S(1)} %copy-done.3, f32[16,128,128]{2,1,0:T(8,128)S(1)} %bitcast.73, f32[4,128,128]{2,1,0:T(8,128)S(1)} %collective-permute-done.7, f32[4,128,128]{2,1,0:T(8,128)S(1)} %collective-permute-done.6, f32[16,128,128]{2,1,0:T(8,128)S(1)} %bitcast.70), kind=kLoop, calls=%fused_computation.142 | loop fusion | flops 10747904 | bytes 4718592 | tf_op jit(solution)/shard_map/add | solution.py:84
  97.0 7.6 %scatter_fusion.3 = f32[262144]{0:T(1024)} fusion(f32[262144]{0:T(1024)} %bitcast.76, s32[1024]{0:T(1024)S(1)} %broadcast_select_fusion, f32[1024]{0:T(1024)S(1)} %get-tuple-element.17), kind=kCustom, calls=%fused_computation.3 | custom fusion | flops 1024 | bytes 16384
  104.6 2.7 %fusion.4 = f32[16,128,128]{2,1,0:T(8,128)S(1)} fusion(f32[16,128,128]{2,1,0:T(8,128)S(1)} %bitcast.74, f32[16,128,128]{2,1,0:T(8,128)S(1)} %bitcast.67, f32[16,128,128]{2,1,0:T(8,128)S(1)} %bitcast.71, f32[16,128,128]{2,1,0:T(8,128)} %bitcast.77, bf16[1,6,16,128,128]{4,3,2,1,0:T(8,128)(2,1)} %param.8, s32[128]{0:T(128)S(1)} %subtract_multiply_fusion, ...), kind=kLoop, calls=%fused_computation.131 | loop fusion | flops 8126464 | bytes 8397312 | tf_op jit(solution)/shard_map/mul | solution.py:125
  107.4 1.1 copy.8
  108.4 3.7 %all-to-all-start = ((f32[4,16,32,128]{3,2,1,0:T(8,128)}), f32[4,16,32,128]{3,2,1,0:T(8,128)S(1)}, u32[]{:S(2)}, u32[]{:S(2)}) async-start(f32[4,16,32,128]{3,2,1,0:T(8,128)} %copy.8), calls=%async_computation | async-start | bytes 2097152 | tf_op jit(solution)/shard_map/all_to_all | solution.py:33
  112.2 1.5 %maximum_bitcast_fusion = f32[1,2,16,128,128]{4,3,2,1,0:T(8,128)} fusion(f32[1,16,128,128]{3,2,1,0:T(8,128)S(1)} %bitcast.78, f32[1,16,128,128]{3,2,1,0:T(8,128)S(1)} %bitcast.75), kind=kLoop, calls=%fused_computation.92 | loop fusion | flops 524288 | bytes 4194304 | tf_op jit(solution)/shard_map/broadcast_in_dim | solution.py:127
  113.7 10.5 %all-to-all-done = f32[4,16,32,128]{3,2,1,0:T(8,128)S(1)} async-done(((f32[4,16,32,128]{3,2,1,0:T(8,128)}), f32[4,16,32,128]{3,2,1,0:T(8,128)S(1)}, u32[]{:S(2)}, u32[]{:S(2)}) %all-to-all-start) | async-done | bytes 1048608 | tf_op jit(solution)/shard_map/all_to_all | solution.py:33
  124.2 0.8 reduce_sum.9
  (9 shorter events, 0.1 us)
Async XLA Ops:
  1.7 29.0 %copy-start.1 = (f32[16,128,128]{2,1,0:T(8,128)S(1)}, f32[16,128,128]{2,1,0:T(8,128)}, u32[]{:S(2)}) copy-start(f32[16,128,128]{2,1,0:T(8,128)} %param.6) | copy-start | bytes 3145732
  1.7 29.0 %collective-permute-start.1 = (f32[4,128,128]{2,1,0:T(8,128)S(1)}, f32[4,128,128]{2,1,0:T(8,128)S(1)}, u32[]{:S(2)}, u32[]{:S(2)}) collective-permute-start(f32[4,128,128]{2,1,0:T(8,128)S(1)} %get-tuple-element.3), channel_id=1, source_target_pairs={{0,4},{4,8},{8,12},{12,16},{16,20},{20,24},{24,28},{28,32},{32,36}... | collective-permute-start | bytes 786440 | tf_op jit(solution)/shard_map/ppermute | solution.py:20
  7.6 23.1 %collective-permute-start = (f32[4,128,128]{2,1,0:T(8,128)S(1)}, f32[4,128,128]{2,1,0:T(8,128)}, u32[]{:S(2)}, u32[]{:S(2)}) collective-permute-start(f32[4,128,128]{2,1,0:T(8,128)S(1)} %get-tuple-element.2), channel_id=1, source_target_pairs={{4,0},{8,4},{12,8},{16,12},{20,16},{24,20},{28,24},{32,28},{36,32}... | collective-permute-start | bytes 786440 | tf_op jit(solution)/shard_map/ppermute | solution.py:21
  41.9 5.3 %collective-permute-start.3 = (f32[4,128,128]{2,1,0:T(8,128)S(1)}, f32[4,128,128]{2,1,0:T(8,128)S(1)}, u32[]{:S(2)}, u32[]{:S(2)}) collective-permute-start(f32[4,128,128]{2,1,0:T(8,128)S(1)} %bitcast.85), channel_id=1, source_target_pairs={{0,4},{4,8},{8,12},{12,16},{16,20},{20,24},{24,28},{28,32},{32,36}... | collective-permute-start | bytes 786440 | tf_op jit(solution)/shard_map/ppermute | solution.py:20
  43.8 7.7 %collective-permute-start.2 = (f32[4,128,128]{2,1,0:T(8,128)S(1)}, f32[4,128,128]{2,1,0:T(8,128)S(1)}, u32[]{:S(2)}, u32[]{:S(2)}) collective-permute-start(f32[4,128,128]{2,1,0:T(8,128)S(1)} %bitcast.84), channel_id=1, source_target_pairs={{4,0},{8,4},{12,8},{16,12},{20,16},{24,20},{28,24},{32,28},{36,32}... | collective-permute-start | bytes 786440 | tf_op jit(solution)/shard_map/ppermute | solution.py:21
  56.3 11.1 %copy-start.4 = (s32[1,3]{1,0:T(1,128)S(1)}, s32[1,3]{1,0:T(1,128)}, u32[]{:S(2)}) copy-start(s32[1,3]{1,0:T(1,128)} %param.11) | copy-start | bytes 40
  62.7 9.9 %copy-start.2 = (f32[16,128,128]{2,1,0:T(8,128)S(1)}, f32[16,128,128]{2,1,0:T(8,128)}, u32[]{:S(2)}) copy-start(f32[16,128,128]{2,1,0:T(8,128)} %param.6) | copy-start | bytes 3145732
  62.8 6.6 %collective-permute-start.5 = (f32[4,128,128]{2,1,0:T(8,128)S(1)}, f32[4,128,128]{2,1,0:T(8,128)S(1)}, u32[]{:S(2)}, u32[]{:S(2)}) collective-permute-start(f32[4,128,128]{2,1,0:T(8,128)S(1)} %bitcast.82), channel_id=1, source_target_pairs={{0,4},{4,8},{8,12},{12,16},{16,20},{20,24},{24,28},{28,32},{32,36}... | collective-permute-start | bytes 786440 | tf_op jit(solution)/shard_map/ppermute | solution.py:20
  64.9 7.7 %collective-permute-start.4 = (f32[4,128,128]{2,1,0:T(8,128)S(1)}, f32[4,128,128]{2,1,0:T(8,128)S(1)}, u32[]{:S(2)}, u32[]{:S(2)}) collective-permute-start(f32[4,128,128]{2,1,0:T(8,128)S(1)} %bitcast.80), channel_id=1, source_target_pairs={{4,0},{8,4},{12,8},{16,12},{20,16},{24,20},{28,24},{32,28},{36,32}... | collective-permute-start | bytes 786440 | tf_op jit(solution)/shard_map/ppermute | solution.py:21
  82.7 9.9 %copy-start.3 = (f32[16,128,128]{2,1,0:T(8,128)S(1)}, f32[16,128,128]{2,1,0:T(8,128)}, u32[]{:S(2)}) copy-start(f32[16,128,128]{2,1,0:T(8,128)} %param.6) | copy-start | bytes 3145732
  82.8 5.5 %collective-permute-start.7 = (f32[4,128,128]{2,1,0:T(8,128)S(1)}, f32[4,128,128]{2,1,0:T(8,128)S(1)}, u32[]{:S(2)}, u32[]{:S(2)}) collective-permute-start(f32[4,128,128]{2,1,0:T(8,128)S(1)} %bitcast.83), channel_id=1, source_target_pairs={{0,4},{4,8},{8,12},{12,16},{16,20},{20,24},{24,28},{28,32},{32,36}... | collective-permute-start | bytes 786440 | tf_op jit(solution)/shard_map/ppermute | solution.py:20
  84.9 7.7 %collective-permute-start.6 = (f32[4,128,128]{2,1,0:T(8,128)S(1)}, f32[4,128,128]{2,1,0:T(8,128)S(1)}, u32[]{:S(2)}, u32[]{:S(2)}) collective-permute-start(f32[4,128,128]{2,1,0:T(8,128)S(1)} %bitcast.81), channel_id=1, source_target_pairs={{4,0},{8,4},{12,8},{16,12},{20,16},{24,20},{28,24},{32,28},{36,32}... | collective-permute-start | bytes 786440 | tf_op jit(solution)/shard_map/ppermute | solution.py:21
  108.4 3.8 %copy-start = (f32[262144]{0:T(1024)S(1)}, f32[262144]{0:T(1024)}, u32[]{:S(2)}) copy-start(f32[262144]{0:T(1024)} %scatter_fusion.3) | copy-start | bytes 3145732
  108.4 15.7 %all-to-all-start = ((f32[4,16,32,128]{3,2,1,0:T(8,128)}), f32[4,16,32,128]{3,2,1,0:T(8,128)S(1)}, u32[]{:S(2)}, u32[]{:S(2)}) async-start(f32[4,16,32,128]{3,2,1,0:T(8,128)} %copy.8), calls=%async_computation | async-start | bytes 2097152 | tf_op jit(solution)/shard_map/all_to_all | solution.py:33
where the time goes:
time: 126 us; the launch traced here: 125 us
  other arithmetic  54.3 us (43%)
  starting transfers between devices  41.2 us (33%)
  waiting for transfers between devices  23.3 us (18%)
  local copies, waits for them, and re-layouts  5.13 us (4%)
    unnamed x7, other arithmetic  28.5 us
    ppermute x4, starting transfers between devices, padded_2(): after = lax.ppermute(initial, axis, down)  25.5 us
    add x4, other arithmetic, advance(): 2.0 * level_now[4:4 + row_count] - level_later[4:4 + row_count]  17.4 us
    ppermute x4, waiting for transfers between devices, padded_2(): after = lax.ppermute(initial, axis, down)  12 us
    ppermute x4, starting transfers between devices, padded_2(): before = lax.ppermute(last, axis, up)  12 us
    all_to_all x1, waiting for transfers between devices, sum_at_owner(): pieces = lax.all_to_all(split_up(array, dim, size), axis, 0, 0, tiled=True)  10.5 us
    all_to_all x1, starting transfers between devices, sum_at_owner(): pieces = lax.all_to_all(split_up(array, dim, size), axis, 0, 0, tiled=True)  3.74 us
    mul x1, other arithmetic, per_device(): source_taper(sources[0], first_row, slab_rows, size_x, size_y) * summed  2.72 us
  transfers between devices with their start and end apart: 9, of which 5 were waited for; matrix products, arithmetic and copies ran while one was open for 7% of the time, Pallas kernels for 0%

commit v1 on v0

v1 whole, which is shorter than its diff:
```python
import functools

import jax
import jax.numpy as jnp
from jax import lax
from jax.experimental import pallas as pl
from jax.experimental.pallas import tpu as pltpu
from jax.sharding import PartitionSpec as P

ITERS = 4
RADIUS = 6
WIDTH = 4
PAD = 8
CHUNKS = 4
BLOCKS = 4
MESH = pl.DeviceIdType.MESH

SCALE = 5040.0
CENTRE = 3.0 * -14350.0
OFFSET = (0.0, 8064.0, -1008.0, 128.0, -9.0)


def kernel(
    planes,
    size_x,
    size_y,
    dom_size,
    courant_hbm,
    adjoint_hbm,
    forward_hbm,
    traces_ref,
    receivers_ref,
    source_ref,
    gradient_ref,
    final_hbm,
    lam0,
    lam1,
    lam2,
    lam3,
    lam4,
    later,
    courant,
    forward,
    along,
    band,
    spots,
    amounts,
    image,
    taper_z,
    taper_xy,
    far_halo,
    near_halo,
    got_first,
    sent_second,
    got_second,
    in_sem,
    out_sem,
    far_send,
    far_recv,
    near_send,
    near_recv,
    first_send,
    first_recv,
    second_send,
    second_recv,
):
    lam = (lam0, lam1, lam2, lam3, lam4)
    dom = lax.axis_index("dom")
    shot = lax.axis_index("shot")
    parity = dom % 2
    first_row = dom * planes
    far = dom + 2 * parity - 1
    near = dom + 1 - 2 * parity
    has_far = (far >= 0) & (far < dom_size)
    shot_a = shot + 1 - 2 * (shot % 2)
    shot_b = 3 - shot
    shot_c = (shot + 2) % 4
    rows = size_x // CHUNKS

    def depth(q):
        return q + parity * (planes - 1 - 2 * q)

    def load(kind, q):
        z = depth(q)
        if kind == 0:
            source, target = adjoint_hbm.at[0, 1, z], lam4.at[q, pl.ds(PAD, size_x)]
        elif kind == 1:
            source, target = adjoint_hbm.at[0, 0, z], later.at[q]
        elif kind == 2:
            source, target = courant_hbm.at[z], courant.at[q]
        else:
            source, target = forward_hbm.at[0, :, z], forward.at[:, q]
        return pltpu.make_async_copy(source, target, in_sem.at[kind, q])

    order = [0, 1, 2, 3] + list(range(planes - 1, 3, -1))
    for kind in range(4):
        for q in order:
            load(kind, q).start()

    barrier = pltpu.get_barrier_semaphore()
    for axis, target in (("dom", near), ("shot", shot_a), ("shot", shot_b)):
        pl.semaphore_signal(barrier, inc=1, device_id={axis: target}, device_id_type=MESH)

    @pl.when(has_far)
    def _():
        pl.semaphore_signal(barrier, inc=1, device_id={"dom": far}, device_id_type=MESH)

    for level in (1, 2, 3, 4):
        for q in range(planes):
            zero = jnp.zeros((PAD, size_y), jnp.float32)
            lam[level][q, pl.ds(0, PAD), :] = zero
            lam[level][q, pl.ds(PAD + size_x, PAD), :] = zero

    @pl.when(jnp.logical_not(has_far))
    def _():
        far_halo[...] = jnp.zeros(far_halo.shape, jnp.float32)

    row = lax.broadcasted_iota(jnp.int32, (2 * size_y, size_y), 0) % size_y
    gap = jnp.abs(row - lax.broadcasted_iota(jnp.int32, (2 * size_y, size_y), 1))
    weights = jnp.zeros(gap.shape, jnp.float32)
    for k in range(1, WIDTH + 1):
        weights = jnp.where(gap == k, OFFSET[k], weights)
    band[...] = weights.astype(jnp.bfloat16)

    @pl.when(has_far)
    def _():
        pl.semaphore_wait(barrier, 4)

    @pl.when(jnp.logical_not(has_far))
    def _():
        pl.semaphore_wait(barrier, 3)

    def far_copy(level, c):
        return pltpu.make_async_remote_copy(
            src_ref=lam[level].at[pl.ds(0, WIDTH), pl.ds(PAD + c * rows, rows)],
            dst_ref=far_halo.at[level - 1, :, pl.ds(c * rows, rows)],
            send_sem=far_send.at[level - 1, c],
            recv_sem=far_recv.at[level - 1, c],
            device_id={"dom": far},
            device_id_type=MESH,
        )

    def near_copy(level):
        return pltpu.make_async_remote_copy(
            src_ref=lam[level].at[pl.ds(planes - WIDTH, WIDTH), pl.ds(PAD, size_x)],
            dst_ref=near_halo.at[level - 1],
            send_sem=near_send.at[level - 1],
            recv_sem=near_recv.at[level - 1],
            device_id={"dom": near},
            device_id_type=MESH,
        )

    def far_start(level, c):
        @pl.when(has_far)
        def _():
            far_copy(level, c).start()

    def far_wait(level, c):
        @pl.when(has_far)
        def _():
            far_copy(level, c).wait_recv()

    for q in range(WIDTH):
        load(0, q).wait()
    for c in range(CHUNKS):
        far_start(4, c)
    for q in range(planes - WIDTH, planes):
        load(0, q).wait()
    near_copy(4).start()
    for q in range(WIDTH, planes - WIDTH):
        load(0, q).wait()

    z_index = receivers_ref[pl.ds(0, 1), :] - first_row
    z_index = z_index + parity * (planes - 1 - 2 * z_index)
    cell_row = z_index * size_x + receivers_ref[pl.ds(1, 1), :]
    count = cell_row.shape[1]

    def spots_of(block):
        base = block * WIDTH * size_x

        def body(i, carry):
            here = base + i * 16
            ids = lax.broadcasted_iota(jnp.int32, (16, count), 0) + here
            hit = jnp.where(ids == cell_row, 1.0, 0.0)
            spots[pl.ds(pl.multiple_of(here, 16), 16), :] = hit.astype(jnp.bfloat16)
            return carry

        lax.fori_loop(0, WIDTH * size_x // 16, body, 0)

    def amounts_of(step):
        value = traces_ref[pl.ds(step, 1), :]
        high = value.astype(jnp.bfloat16).astype(jnp.float32)
        low = value - high
        last = receivers_ref[pl.ds(2, 1), :]

        def body(i, carry):
            ids = lax.broadcasted_iota(jnp.int32, (16, count), 0) + i * 16
            hit = ids == last
            start = pl.multiple_of(i * 16, 16)
            amounts[step, pl.ds(start, 16), :] = jnp.where(hit, high, 0.0).astype(jnp.bfloat16)
            amounts[step, pl.ds(size_y + start, 16), :] = jnp.where(hit, low, 0.0).astype(jnp.bfloat16)
            return carry

        lax.fori_loop(0, size_y // 16, body, 0)

    def inject(step, block):
        cells = WIDTH * size_x
        both = lax.dot_general(
            spots[pl.ds(block * cells, cells), :],
            amounts[step],
            (((1,), (1,)), ((), ())),
            preferred_element_type=jnp.float32,
        )
        added = both[:, :size_y] + both[:, size_y:]
        lam[step][pl.ds(block * WIDTH, WIDTH), pl.ds(PAD, size_x), :] = added.reshape(WIDTH, size_x, size_y)

    def lateral(level, block, start, length):
        planes_here = pl.ds(block * WIDTH, WIDTH)
        field = lam[level][planes_here, pl.ds(PAD + start, length), :].reshape(WIDTH * length, size_y)
        high = field.astype(jnp.bfloat16)
        low = (field - high.astype(jnp.float32)).astype(jnp.bfloat16)
        result = jnp.dot(
            jnp.concatenate([high, low], axis=1), band[...], preferred_element_type=jnp.float32
        )
        along[planes_here, pl.ds(start, length), :] = result.reshape(WIDTH, length, size_y)

    def advance(step, block, start=0, length=size_x):
        now = lam[step + 1]
        before = later if step == 3 else lam[step + 2]
        offset = 0 if step == 3 else PAD
        low, high = block * WIDTH, (block + 1) * WIDTH
        lateral(step + 1, block, start, length)

        def body(i, carry):
            at = start + i * 8
            here = pl.ds(pl.multiple_of(at, 8), 8)
            padded = pl.ds(pl.multiple_of(at + PAD, 8), 8)
            column = {}
            for q in range(low - WIDTH, high + WIDTH):
                if 0 <= q < planes:
                    column[q] = now[q, padded, :]
                elif q >= planes:
                    column[q] = near_halo[step, WIDTH - 1 - (q - planes), here, :]
            for q in range(low, high):
                centre = column[q]
                total = along[q, here, :] + CENTRE * centre
                for k in range(1, WIDTH + 1):
                    beside = now[q, pl.ds(at + PAD + k, 8), :] + now[q, pl.ds(at + PAD - k, 8), :]
                    beside = beside + column[q + k]
                    if q - k >= 0:
                        beside = beside + column[q - k]
                    total = total + OFFSET[k] * beside
                moved = 2.0 * centre - before[q, pl.ds(pl.multiple_of(at + offset, 8), 8), :]
                scaled = courant[q, here, :] * (1.0 / SCALE)
                lam[step][q, padded, :] = lam[step][q, padded, :] + (moved + scaled * total)
            return carry

        lax.fori_loop(0, length // 8, body, 0)

    def finish(step, c):
        def body(i, carry):
            at = c * rows + i * 8
            here = pl.ds(pl.multiple_of(at, 8), 8)
            padded = pl.ds(pl.multiple_of(at + PAD, 8), 8)
            beyond = [far_halo[step, d, here, :] for d in range(WIDTH)]
            for q in range(WIDTH):
                total = OFFSET[q + 1] * beyond[0]
                for d in range(1, WIDTH - q):
                    total = total + OFFSET[q + 1 + d] * beyond[d]
                scaled = courant[q, here, :] * (1.0 / SCALE)
                lam[step][q, padded, :] = lam[step][q, padded, :] + scaled * total
            return carry

        lax.fori_loop(0, rows // 8, body, 0)

    def imaging(block):
        def body(i, carry):
            at = pl.multiple_of(i * 16, 16)
            here = pl.ds(at, 16)
            padded = pl.ds(pl.multiple_of(at + PAD, 8), 16)
            across = taper_xy[here, :]
            for q in range(block * WIDTH, (block + 1) * WIDTH):
                saved = [forward[j, q, here, :].astype(jnp.float32) for j in range(ITERS + 2)]
                total = None
                for step in range(ITERS):
                    accel = saved[step + 2] - 2.0 * saved[step + 1] + saved[step]
                    term = lam[step][q, padded, :] * accel
                    total = term if total is None else total + term
                image[q, here, :] = total * (1.0 - taper_z[pl.ds(q, 1), :] * across)
            return carry

        lax.fori_loop(0, size_x // 16, body, 0)

    piece = size_x // 4

    def first_copy(block, side, which):
        q = block * WIDTH + 2 * side
        target = (shot_a, shot_b)[side]
        part = (target, shot_c)[which]
        return pltpu.make_async_remote_copy(
            src_ref=image.at[pl.ds(q, 2), pl.ds(pl.multiple_of(part * piece, 8), piece)],
            dst_ref=got_first.at[block, side, which],
            send_sem=first_send.at[block, side, which],
            recv_sem=first_recv.at[block, side, which],
            device_id={"shot": target},
            device_id_type=MESH,
        )

    def second_copy(block, side):
        return pltpu.make_async_remote_copy(
            src_ref=sent_second.at[block, side],
            dst_ref=got_second.at[block, side],
            send_sem=second_send.at[block, side],
            recv_sem=second_recv.at[block, side],
            device_id={"shot": (shot_b, shot_a)[side]},
            device_id_type=MESH,
        )

    def reduce_start(block):
        for side in range(2):
            for which in (1, 0):
                first_copy(block, side, which).start()

    def reduce_next(block):
        for side in range(2):
            onward = (shot_b, shot_a)[side]
            q = block * WIDTH + 2 * side
            first_copy(block, side, 1).wait_recv()
            sent_second[block, side] = (
                image[pl.ds(q, 2), pl.ds(pl.multiple_of(onward * piece, 8), piece), :]
                + got_first[block, side, 1]
            )
            second_copy(block, side).start()

    def reduce_end(block):
        for side in range(2):
            first_copy(block, side, 0).wait_recv()
            second_copy(block, side).wait_recv()
            q = block * WIDTH + 2 * side
            own = image[pl.ds(q, 2), pl.ds(pl.multiple_of(shot * piece, 8), piece), :]
            own = own + got_first[block, side, 0] + got_second[block, side]
            for j in range(2):
                gradient_ref[depth(q + j)] = own[j]

    def store(level, q):
        return pltpu.make_async_copy(
            lam[level].at[q, pl.ds(PAD, size_x)], final_hbm.at[0, 1 - level, depth(q)], out_sem.at[level, q]
        )

    def store_block(level, block):
        for q in range(block * WIDTH, (block + 1) * WIDTH):
            store(level, q).start()

    def tapers():
        q_index = lax.broadcasted_iota(jnp.int32, (planes, size_y), 0)
        z_gap = q_index + parity * (planes - 1 - 2 * q_index) + first_row - source_ref[0, 0]
        taper_z[...] = jnp.exp((z_gap * z_gap).astype(jnp.float32) * (-1.0 / (RADIUS * RADIUS)))
        x_gap = lax.broadcasted_iota(jnp.int32, (size_x, size_y), 0) - source_ref[0, 1]
        y_gap = lax.broadcasted_iota(jnp.int32, (size_x, size_y), 1) - source_ref[0, 2]
        square = x_gap * x_gap + y_gap * y_gap
        taper_xy[...] = jnp.exp(square.astype(jnp.float32) * (-1.0 / (RADIUS * RADIUS)))

    amounts_of(3)
    spots_of(0)
    inject(3, 0)
    for kind in (1, 2):
        for q in order:
            load(kind, q).wait()
    advance(3, 0)
    spots_of(3)
    inject(3, 3)
    near_copy(4).wait_recv()
    advance(3, 3)
    near_copy(3).start()
    spots_of(2)
    inject(3, 2)
    advance(3, 2)
    spots_of(1)
    inject(3, 1)
    advance(3, 1)

    def wave(step, fills):
        for c in range(CHUNKS):
            far_wait(step + 1, c)
            finish(step, c)
            if step > 0:
                far_start(step, c)
                if c > 0:
                    advance(step - 1, 0, (c - 1) * rows, rows)
            if c == CHUNKS - 1 and step > 0:
                advance(step - 1, 0, c * rows, rows)
            for fill in fills[c]:
                fill()

    def full(step, block):
        inject(step, block)
        advance(step, block)

    def edge(step):
        near_copy(step + 1).wait_recv()
        full(step, 3)
        if step > 0:
            near_copy(step).start()

    def wait_forward():
        for q in order:
            load(3, q).wait()

    amounts_of(2)
    inject(2, 0)
    wave(
        3,
        [
            [lambda: edge(2)],
            [lambda: full(2, 2), lambda: amounts_of(1)],
            [lambda: edge(1), tapers],
            [lambda: inject(1, 0), lambda: full(2, 1)],
        ],
    )
    wave(
        2,
        [
            [lambda: full(1, 2), lambda: amounts_of(0)],
            [lambda: edge(0), wait_forward],
            [lambda: imaging(3), lambda: reduce_start(3)],
            [lambda: inject(0, 0), lambda: full(1, 1), lambda: reduce_next(3)],
        ],
    )
    wave(
        1,
        [
            [lambda: full(0, 2)],
            [lambda: imaging(2), lambda: reduce_start(2)],
            [lambda: reduce_end(3)],
            [lambda: full(0, 1), lambda: imaging(1), lambda: reduce_start(1), lambda: reduce_next(2)],
        ],
    )
    for block in range(BLOCKS):
        store_block(1, block)
    for block in range(1, BLOCKS):
        store_block(0, block)
    wave(0, [[lambda: reduce_next(1)], [lambda: reduce_end(2)], [], []])
    store_block(0, 0)
    imaging(0)
    reduce_start(0)
    reduce_end(1)
    reduce_next(0)
    reduce_end(0)

    for level in (1, 2, 3, 4):
        near_copy(level).wait_send()

        @pl.when(has_far)
        def _():
            for c in range(CHUNKS):
                far_copy(level, c).wait_send()

    for block in range(BLOCKS):
        for side in range(2):
            first_copy(block, side, 0).wait_send()
            first_copy(block, side, 1).wait_send()
            second_copy(block, side).wait_send()
    for level in range(2):
        for q in range(planes):
            store(level, q).wait()


def per_device(dom_size, courant_sq, adjoint_init, forward_saved, residual_traces, receivers, sources):
    planes, size_x, size_y = courant_sq.shape
    count = receivers.shape[1]
    f32, bf16 = jnp.float32, jnp.bfloat16
    padded = pltpu.VMEM((planes, size_x + 2 * PAD, size_y), f32)
    grid3 = (planes, size_x, size_y)
    dma = pltpu.SemaphoreType.DMA
    piece = (2, size_x // 4, size_y)
    return pl.pallas_call(
        functools.partial(kernel, planes, size_x, size_y, dom_size),
        out_shape=(
            jax.ShapeDtypeStruct((planes, size_x // 4, size_y), f32),
            jax.ShapeDtypeStruct((1, 2, planes, size_x, size_y), f32),
        ),
        in_specs=[pl.BlockSpec(memory_space=pl.ANY)] * 3
        + [pl.BlockSpec(memory_space=pltpu.VMEM)] * 2
        + [pl.BlockSpec(memory_space=pltpu.SMEM)],
        out_specs=(pl.BlockSpec(memory_space=pltpu.VMEM), pl.BlockSpec(memory_space=pl.ANY)),
        scratch_shapes=[padded] * 5
        + [
            pltpu.VMEM(grid3, f32),
            pltpu.VMEM(grid3, f32),
            pltpu.VMEM((ITERS + 2,) + grid3, bf16),
            pltpu.VMEM(grid3, f32),
            pltpu.VMEM((2 * size_y, size_y), bf16),
            pltpu.VMEM((planes * size_x, count), bf16),
            pltpu.VMEM((ITERS, 2 * size_y, count), bf16),
            pltpu.VMEM(grid3, f32),
            pltpu.VMEM((planes, size_y), f32),
            pltpu.VMEM((size_x, size_y), f32),
            pltpu.VMEM((ITERS, WIDTH, size_x, size_y), f32),
            pltpu.VMEM((ITERS, WIDTH, size_x, size_y), f32),
            pltpu.VMEM((BLOCKS, 2, 2) + piece, f32),
            pltpu.VMEM((BLOCKS, 2) + piece, f32),
            pltpu.VMEM((BLOCKS, 2) + piece, f32),
            dma((4, planes)),
            dma((2, planes)),
            dma((ITERS, CHUNKS)),
            dma((ITERS, CHUNKS)),
            dma((ITERS,)),
            dma((ITERS,)),
            dma((BLOCKS, 2, 2)),
            dma((BLOCKS, 2, 2)),
            dma((BLOCKS, 2)),
            dma((BLOCKS, 2)),
        ],
        compiler_params=pltpu.CompilerParams(
            collective_id=0, has_side_effects=True, vmem_limit_bytes=60 * 1024 * 1024
        ),
    )(courant_sq, adjoint_init, forward_saved, residual_traces[0], receivers[0].T, sources)


def solution(mesh):
    placed = (
        P(("groups", "dom"), None, None),
        P(("groups", "shot"), None, "dom", None, None),
        P(("groups", "shot"), None, "dom", None, None),
        P(("groups", "shot"), None, None),
        P(("groups", "shot"), None, None),
        P(("groups", "shot"), None),
    )
    return jax.shard_map(
        functools.partial(per_device, mesh.shape["dom"]),
        mesh=mesh,
        in_specs=placed,
        out_specs=(
            P(("groups", "dom"), "shot", None),
            P(("groups", "shot"), None, "dom", None, None),
        ),
        check_vma=False,
    )
```

time: 126 us -> 66.5 us (0.53)
  the two profiles are of different devices: /device:TPU:33 before, /device:TPU:36 now
where the time goes in v1:
time: 66.5 us; the launch traced here: 66.3 us
  Pallas kernels  59.5 us (89%)
  local copies, waits for them, and re-layouts  6.12 us (9%)
    pallas_call x1, Pallas kernels, per_device(): pl.pallas_call(functools.partial(kernel, planes, size_x, size_y, dom_size...  59.5 us
    unnamed x3, local copies, waits for them, and re-layouts  6.12 us

profile of v1, /device:TPU:36, one launch (start us, length us, event | category | flops | bytes accessed | tf_op | source)
XLA Modules:
  0.0 66.3 jit_solution(4153347952252769167)
XLA Ops:
  0.6 1.3 %copy.10 = s32[1,1024,3]{1,2,0:T(4,128)} copy(s32[1,1024,3]{1,0,2:T(1,128)} %param.10) | data formatting | bytes 24576
  1.9 59.5 %shard_map.77 = (f32[16,32,128]{2,1,0:T(8,128)}, f32[1,2,16,128,128]{4,3,2,1,0:T(8,128)}) custom-call(f32[16,128,128]{2,1,0:T(8,128)} %courant_hbm.1, f32[1,2,16,128,128]{4,3,2,1,0:T(8,128)} %adjoint_hbm.1, bf16[1,6,16,128,128]{4,3,2,1,0:T(8,128)(2,1)} %forward_hbm.1, f32[4,1024]{1,0:T(4,128)} %bitcast.7, s32[3,1024]{1,0:T(4,128)} %bitcast.6, s32[1,3]{1,0:T(1,128)} %source_ref.1), custom_call_target="tpu_custom_call" | custom-call | tf_op jit(solution)/shard_map/pallas_call | solution.py:476
  61.5 1.7 %copy.13 = f32[16,32,128]{2,1,0:T(8,128)} copy(f32[16,32,128]{2,1,0:T(8,128)} %get-tuple-element.4) | data formatting | bytes 524288
  63.1 3.1 %copy.14 = f32[1,2,16,128,128]{4,3,2,1,0:T(8,128)} copy(f32[1,2,16,128,128]{4,3,2,1,0:T(8,128)} %get-tuple-element.5) | data formatting | bytes 4194304

commit v2 on v1

--- a/solution.py
+++ b/solution.py
@@ -11,9 +11,13 @@
 RADIUS = 6
 WIDTH = 4
 PAD = 8
-CHUNKS = 4
+CHUNKS = 2
 BLOCKS = 4
 MESH = pl.DeviceIdType.MESH
+
+
+def in_hbm(array):
+    return pltpu.with_memory_space_constraint(array, pltpu.HBM)
 
 SCALE = 5040.0
 CENTRE = 3.0 * -14350.0
@@ -28,11 +32,14 @@
     courant_hbm,
     adjoint_hbm,
     forward_hbm,
+    traces_hbm,
+    receivers_hbm,
+    source_hbm,
+    gradient_ref,
+    final_ref,
     traces_ref,
     receivers_ref,
     source_ref,
-    gradient_ref,
-    final_hbm,
     lam0,
     lam1,
     lam2,
@@ -54,7 +61,7 @@
     sent_second,
     got_second,
     in_sem,
-    out_sem,
+    table_sem,
     far_send,
     far_recv,
     near_send,
@@ -76,6 +83,7 @@
     shot_b = 3 - shot
     shot_c = (shot + 2) % 4
     rows = size_x // CHUNKS
+    zero_row = (dom // dom_size) * 8
 
     def depth(q):
         return q + parity * (planes - 1 - 2 * q)
@@ -92,6 +100,14 @@
             source, target = forward_hbm.at[0, :, z], forward.at[:, q]
         return pltpu.make_async_copy(source, target, in_sem.at[kind, q])
 
+    tables = [
+        pltpu.make_async_copy(source, target, table_sem.at[i])
+        for i, (source, target) in enumerate(
+            ((receivers_hbm, receivers_ref), (traces_hbm, traces_ref), (source_hbm, source_ref))
+        )
+    ]
+    for table in tables:
+        table.start()
     order = [0, 1, 2, 3] + list(range(planes - 1, 3, -1))
     for kind in range(4):
         for q in order:
@@ -121,6 +137,53 @@
     for k in range(1, WIDTH + 1):
         weights = jnp.where(gap == k, OFFSET[k], weights)
     band[...] = weights.astype(jnp.bfloat16)
+
+    for table in tables:
+        table.wait()
+
+    z_index = receivers_ref[0] - first_row
+    z_index = z_index + parity * (planes - 1 - 2 * z_index)
+    cell_row = z_index * size_x + receivers_ref[1]
+    count = cell_row.shape[1]
+
+    def spots_of():
+        def body(i, carry):
+            ids = lax.broadcasted_iota(jnp.int32, (16, count), 0) + i * 16
+            hit = jnp.where(ids == cell_row, 1.0, 0.0)
+            spots[pl.ds(pl.multiple_of(i * 16, 16), 16), :] = hit.astype(jnp.bfloat16)
+            return carry
+
+        lax.fori_loop(0, planes * size_x // 16, body, 0)
+
+    def amounts_of(step):
+        value = traces_ref[pl.ds(step, 1), :]
+        high = value.astype(jnp.bfloat16).astype(jnp.float32)
+        low = value - high
+        last = receivers_ref[2]
+
+        def body(i, carry):
+            ids = lax.broadcasted_iota(jnp.int32, (16, count), 0) + i * 16
+            hit = ids == last
+            start = pl.multiple_of(i * 16, 16)
+            amounts[step, pl.ds(start, 16), :] = jnp.where(hit, high, 0.0).astype(jnp.bfloat16)
+            amounts[step, pl.ds(size_y + start, 16), :] = jnp.where(hit, low, 0.0).astype(jnp.bfloat16)
+            return carry
+
+        lax.fori_loop(0, size_y // 16, body, 0)
+
+    def tapers():
+        q_index = lax.broadcasted_iota(jnp.int32, (planes, size_y), 0)
+        z_gap = q_index + parity * (planes - 1 - 2 * q_index) + first_row - source_ref[0, 0]
+        taper_z[...] = jnp.exp((z_gap * z_gap).astype(jnp.float32) * (-1.0 / (RADIUS * RADIUS)))
+        x_gap = lax.broadcasted_iota(jnp.int32, (size_x, size_y), 0) - source_ref[0, 1]
+        y_gap = lax.broadcasted_iota(jnp.int32, (size_x, size_y), 1) - source_ref[0, 2]
+        square = x_gap * x_gap + y_gap * y_gap
+        taper_xy[...] = jnp.exp(square.astype(jnp.float32) * (-1.0 / (RADIUS * RADIUS)))
+
+    spots_of()
+    for step in range(ITERS):
+        amounts_of(step)
+    tapers()
 
     @pl.when(has_far)
     def _():
@@ -167,72 +230,32 @@
     for q in range(planes - WIDTH, planes):
         load(0, q).wait()
     near_copy(4).start()
-    for q in range(WIDTH, planes - WIDTH):
-        load(0, q).wait()
-
-    z_index = receivers_ref[pl.ds(0, 1), :] - first_row
-    z_index = z_index + parity * (planes - 1 - 2 * z_index)
-    cell_row = z_index * size_x + receivers_ref[pl.ds(1, 1), :]
-    count = cell_row.shape[1]
-
-    def spots_of(block):
-        base = block * WIDTH * size_x
-
-        def body(i, carry):
-            here = base + i * 16
-            ids = lax.broadcasted_iota(jnp.int32, (16, count), 0) + here
-            hit = jnp.where(ids == cell_row, 1.0, 0.0)
-            spots[pl.ds(pl.multiple_of(here, 16), 16), :] = hit.astype(jnp.bfloat16)
-            return carry
-
-        lax.fori_loop(0, WIDTH * size_x // 16, body, 0)
-
-    def amounts_of(step):
-        value = traces_ref[pl.ds(step, 1), :]
-        high = value.astype(jnp.bfloat16).astype(jnp.float32)
-        low = value - high
-        last = receivers_ref[pl.ds(2, 1), :]
-
-        def body(i, carry):
-            ids = lax.broadcasted_iota(jnp.int32, (16, count), 0) + i * 16
-            hit = ids == last
-            start = pl.multiple_of(i * 16, 16)
-            amounts[step, pl.ds(start, 16), :] = jnp.where(hit, high, 0.0).astype(jnp.bfloat16)
-            amounts[step, pl.ds(size_y + start, 16), :] = jnp.where(hit, low, 0.0).astype(jnp.bfloat16)
-            return carry
-
-        lax.fori_loop(0, size_y // 16, body, 0)
-
-    def inject(step, block):
-        cells = WIDTH * size_x
+
+    def inject(step):
         both = lax.dot_general(
-            spots[pl.ds(block * cells, cells), :],
-            amounts[step],
-            (((1,), (1,)), ((), ())),
-            preferred_element_type=jnp.float32,
+            spots[...], amounts[step], (((1,), (1,)), ((), ())), preferred_element_type=jnp.float32
         )
         added = both[:, :size_y] + both[:, size_y:]
-        lam[step][pl.ds(block * WIDTH, WIDTH), pl.ds(PAD, size_x), :] = added.reshape(WIDTH, size_x, size_y)
-
-    def lateral(level, block, start, length):
-        planes_here = pl.ds(block * WIDTH, WIDTH)
-        field = lam[level][planes_here, pl.ds(PAD + start, length), :].reshape(WIDTH * length, size_y)
+        lam[step][:, pl.ds(PAD, size_x), :] = added.reshape(planes, size_x, size_y)
+
+    def lateral(level, first, last):
+        here = pl.ds(first * WIDTH, (last - first) * WIDTH)
+        shape = ((last - first) * WIDTH, size_x, size_y)
+        field = lam[level][here, pl.ds(PAD, size_x), :].reshape(-1, size_y)
         high = field.astype(jnp.bfloat16)
         low = (field - high.astype(jnp.float32)).astype(jnp.bfloat16)
         result = jnp.dot(
             jnp.concatenate([high, low], axis=1), band[...], preferred_element_type=jnp.float32
         )
-        along[planes_here, pl.ds(start, length), :] = result.reshape(WIDTH, length, size_y)
-
-    def advance(step, block, start=0, length=size_x):
+        along[here, :, :] = result.reshape(shape)
+
+    def advance(step, block):
         now = lam[step + 1]
         before = later if step == 3 else lam[step + 2]
         offset = 0 if step == 3 else PAD
         low, high = block * WIDTH, (block + 1) * WIDTH
-        lateral(step + 1, block, start, length)
-
-        def body(i, carry):
-            at = start + i * 8
+        for i in range(size_x // 8):
+            at = zero_row + i * 8
             here = pl.ds(pl.multiple_of(at, 8), 8)
             padded = pl.ds(pl.multiple_of(at + PAD, 8), 8)
             column = {}
@@ -253,13 +276,10 @@
                 moved = 2.0 * centre - before[q, pl.ds(pl.multiple_of(at + offset, 8), 8), :]
                 scaled = courant[q, here, :] * (1.0 / SCALE)
                 lam[step][q, padded, :] = lam[step][q, padded, :] + (moved + scaled * total)
-            return carry
-
-        lax.fori_loop(0, length // 8, body, 0)
 
     def finish(step, c):
-        def body(i, carry):
-            at = c * rows + i * 8
+        for i in range(rows // 8):
+            at = zero_row + c * rows + i * 8
             here = pl.ds(pl.multiple_of(at, 8), 8)
             padded = pl.ds(pl.multiple_of(at + PAD, 8), 8)
             beyond = [far_halo[step, d, here, :] for d in range(WIDTH)]
@@ -269,9 +289,6 @@
                     total = total + OFFSET[q + 1 + d] * beyond[d]
                 scaled = courant[q, here, :] * (1.0 / SCALE)
                 lam[step][q, padded, :] = lam[step][q, padded, :] + scaled * total
-            return carry
-
-        lax.fori_loop(0, rows // 8, body, 0)
 
     def imaging(block):
         def body(i, carry):
@@ -342,109 +359,101 @@
             for j in range(2):
                 gradient_ref[depth(q + j)] = own[j]
 
-    def store(level, q):
-        return pltpu.make_async_copy(
-            lam[level].at[q, pl.ds(PAD, size_x)], final_hbm.at[0, 1 - level, depth(q)], out_sem.at[level, q]
-        )
-
-    def store_block(level, block):
+    def store(level, block):
         for q in range(block * WIDTH, (block + 1) * WIDTH):
-            store(level, q).start()
-
-    def tapers():
-        q_index = lax.broadcasted_iota(jnp.int32, (planes, size_y), 0)
-        z_gap = q_index + parity * (planes - 1 - 2 * q_index) + first_row - source_ref[0, 0]
-        taper_z[...] = jnp.exp((z_gap * z_gap).astype(jnp.float32) * (-1.0 / (RADIUS * RADIUS)))
-        x_gap = lax.broadcasted_iota(jnp.int32, (size_x, size_y), 0) - source_ref[0, 1]
-        y_gap = lax.broadcasted_iota(jnp.int32, (size_x, size_y), 1) - source_ref[0, 2]
-        square = x_gap * x_gap + y_gap * y_gap
-        taper_xy[...] = jnp.exp(square.astype(jnp.float32) * (-1.0 / (RADIUS * RADIUS)))
-
-    amounts_of(3)
-    spots_of(0)
-    inject(3, 0)
-    for kind in (1, 2):
-        for q in order:
-            load(kind, q).wait()
-    advance(3, 0)
-    spots_of(3)
-    inject(3, 3)
-    near_copy(4).wait_recv()
-    advance(3, 3)
-    near_copy(3).start()
-    spots_of(2)
-    inject(3, 2)
-    advance(3, 2)
-    spots_of(1)
-    inject(3, 1)
-    advance(3, 1)
-
-    def wave(step, fills):
-        for c in range(CHUNKS):
+            final_ref[1 - level, depth(q)] = lam[level][q, pl.ds(PAD, size_x), :]
+
+    def wait_near(level):
+        near_copy(level).wait_recv()
+
+    def wave(step, first, second):
+        for c, fill in enumerate((first, second)):
             far_wait(step + 1, c)
             finish(step, c)
             if step > 0:
                 far_start(step, c)
-                if c > 0:
-                    advance(step - 1, 0, (c - 1) * rows, rows)
-            if c == CHUNKS - 1 and step > 0:
-                advance(step - 1, 0, c * rows, rows)
-            for fill in fills[c]:
-                fill()
-
-    def full(step, block):
-        inject(step, block)
-        advance(step, block)
-
-    def edge(step):
-        near_copy(step + 1).wait_recv()
-        full(step, 3)
-        if step > 0:
-            near_copy(step).start()
-
-    def wait_forward():
+            fill()
+
+    inject(3)
+    for q in range(WIDTH, planes - WIDTH):
+        load(0, q).wait()
+    for kind in (1, 2):
+        for q in order:
+            load(kind, q).wait()
+    lateral(4, 0, 4)
+    advance(3, 0)
+    advance(3, 2)
+    wait_near(4)
+    advance(3, 3)
+    near_copy(3).start()
+    advance(3, 1)
+
+    def first_3():
+        lateral(3, 1, 4)
+        inject(2)
+        advance(2, 2)
+        wait_near(3)
+        advance(2, 3)
+        near_copy(2).start()
+
+    def second_3():
+        lateral(3, 0, 1)
+        inject(1)
+        advance(2, 0)
+        lateral(2, 3, 4)
+        advance(2, 1)
+        wait_near(2)
+        advance(1, 3)
+        near_copy(1).start()
+
+    def first_2():
+        lateral(2, 1, 3)
+        inject(0)
+        advance(1, 2)
         for q in order:
             load(3, q).wait()
 
-    amounts_of(2)
-    inject(2, 0)
-    wave(
-        3,
-        [
-            [lambda: edge(2)],
-            [lambda: full(2, 2), lambda: amounts_of(1)],
-            [lambda: edge(1), tapers],
-            [lambda: inject(1, 0), lambda: full(2, 1)],
-        ],
-    )
-    wave(
-        2,
-        [
-            [lambda: full(1, 2), lambda: amounts_of(0)],
-            [lambda: edge(0), wait_forward],
-            [lambda: imaging(3), lambda: reduce_start(3)],
-            [lambda: inject(0, 0), lambda: full(1, 1), lambda: reduce_next(3)],
-        ],
-    )
-    wave(
-        1,
-        [
-            [lambda: full(0, 2)],
-            [lambda: imaging(2), lambda: reduce_start(2)],
-            [lambda: reduce_end(3)],
-            [lambda: full(0, 1), lambda: imaging(1), lambda: reduce_start(1), lambda: reduce_next(2)],
-        ],
-    )
-    for block in range(BLOCKS):
-        store_block(1, block)
-    for block in range(1, BLOCKS):
-        store_block(0, block)
-    wave(0, [[lambda: reduce_next(1)], [lambda: reduce_end(2)], [], []])
-    store_block(0, 0)
+    def second_2():
+        lateral(2, 0, 1)
+        lateral(1, 3, 4)
+        advance(1, 0)
+        advance(1, 1)
+        wait_near(1)
+        advance(0, 3)
+        imaging(3)
+        reduce_start(3)
+
+    def first_1():
+        lateral(1, 1, 3)
+        advance(0, 2)
+        imaging(2)
+        reduce_start(2)
+        reduce_next(3)
+
+    def second_1():
+        lateral(1, 0, 1)
+        advance(0, 1)
+        imaging(1)
+        reduce_start(1)
+        advance(0, 0)
+        reduce_next(2)
+        for block in range(1, BLOCKS):
+            store(0, block)
+
+    wave(3, first_3, second_3)
+    wave(2, first_2, second_2)
+    wave(1, first_1, second_1)
+    wave(0, lambda: None, lambda: None)
     imaging(0)
     reduce_start(0)
+    store(0, 0)
+    for block in range(BLOCKS):
+        store(1, block)
+    reduce_end(3)
+    reduce_next(1)
+    reduce_end(2)
+    reduce_next(0)
     reduce_end(1)
-    reduce_next(0)
     reduce_end(0)
 
     for level in (1, 2, 3, 4):
@@ -460,9 +469,22 @@
             first_copy(block, side, 0).wait_send()
             first_copy(block, side, 1).wait_send()
             second_copy(block, side).wait_send()
+
+def write_out(gradient_ref, final_ref, gradient_hbm, final_hbm, sem):
+    copies = [pltpu.make_async_copy(gradient_ref, gradient_hbm, sem.at[0])]
+    half = final_ref.shape[1] // 2
     for level in range(2):
-        for q in range(planes):
-            store(level, q).wait()
+        for part in range(2):
+            at = pl.ds(part * half, half)
+            copies.append(
+                pltpu.make_async_copy(
+                    final_ref.at[level, at], final_hbm.at[0, level, at], sem.at[1 + 2 * level + part]
+                )
+            )
+    for copy in copies:
+        copy.start()
+    for copy in copies:
+        copy.wait()
 
 
 def per_device(dom_size, courant_sq, adjoint_init, forward_saved, residual_traces, receivers, sources):
@@ -473,17 +495,20 @@
     grid3 = (planes, size_x, size_y)
     dma = pltpu.SemaphoreType.DMA
     piece = (2, size_x // 4, size_y)
-    return pl.pallas_call(
+    gradient, final = pl.pallas_call(
         functools.partial(kernel, planes, size_x, size_y, dom_size),
         out_shape=(
             jax.ShapeDtypeStruct((planes, size_x // 4, size_y), f32),
-            jax.ShapeDtypeStruct((1, 2, planes, size_x, size_y), f32),
+            jax.ShapeDtypeStruct((2, planes, size_x, size_y), f32),
         ),
-        in_specs=[pl.BlockSpec(memory_space=pl.ANY)] * 3
-        + [pl.BlockSpec(memory_space=pltpu.VMEM)] * 2
-        + [pl.BlockSpec(memory_space=pltpu.SMEM)],
-        out_specs=(pl.BlockSpec(memory_space=pltpu.VMEM), pl.BlockSpec(memory_space=pl.ANY)),
-        scratch_shapes=[padded] * 5
+        in_specs=[pl.BlockSpec(memory_space=pltpu.HBM)] * 6,
+        out_specs=(pl.BlockSpec(memory_space=pltpu.VMEM), pl.BlockSpec(memory_space=pltpu.VMEM)),
+        scratch_shapes=[
+            pltpu.VMEM((ITERS, count), f32),
+            pltpu.VMEM((3, 1, count), jnp.int32),
+            pltpu.SMEM((1, 3), jnp.int32),
+        ]
+        + [padded] * 5
         + [
             pltpu.VMEM(grid3, f32),
             pltpu.VMEM(grid3, f32),
@@ -501,7 +526,7 @@
             pltpu.VMEM((BLOCKS, 2) + piece, f32),
             pltpu.VMEM((BLOCKS, 2) + piece, f32),
             dma((4, planes)),
-            dma((2, planes)),
+            dma((3,)),
             dma((ITERS, CHUNKS)),
             dma((ITERS, CHUNKS)),
             dma((ITERS,)),
@@ -512,9 +537,32 @@
             dma((BLOCKS, 2)),
         ],
         compiler_params=pltpu.CompilerParams(
-            collective_id=0, has_side_effects=True, vmem_limit_bytes=60 * 1024 * 1024
+            collective_id=0, has_side_effects=True, vmem_limit_bytes=34 * 1024 * 1024
         ),
-    )(courant_sq, adjoint_init, forward_saved, residual_traces[0], receivers[0].T, sources)
+    )(
+        *(
+            in_hbm(array)
+            for array in (
+                courant_sq,
+                adjoint_init,
+                forward_saved,
+                residual_traces[0],
+                receivers.transpose(2, 0, 1),
+                sources,
+            )
+        )
+    )
+    return pl.pallas_call(
+        write_out,
+        out_shape=(
+            jax.ShapeDtypeStruct(gradient.shape, f32),
+            jax.ShapeDtypeStruct((1,) + final.shape, f32),
+        ),
+        in_specs=[pl.BlockSpec(memory_space=pltpu.VMEM)] * 2,
+        out_specs=(pl.BlockSpec(memory_space=pl.ANY),) * 2,
+        scratch_shapes=[dma((5,))],
+        compiler_params=pltpu.CompilerParams(vmem_limit_bytes=8 * 1024 * 1024),
+    )(gradient, final)
 
 
 def solution(mesh):

time: 66.5 us -> 54.2 us (0.82)
  the two profiles are of different devices: /device:TPU:36 before, /device:TPU:34 now
where the time goes in v2:
time: 54.2 us; the launch traced here: 54.1 us
  Pallas kernels  53.3 us (98%)
  between operations  0.8 us (1%)
    pallas_call x1, Pallas kernels, per_device(): pl.pallas_call(functools.partial(kernel, planes, size_x, size_y, dom_size...  51.9 us
    pallas_call x1, Pallas kernels, per_device(): pl.pallas_call(write_out, out_shape=(jax.ShapeDtypeStruct(gradient.shape,...  1.44 us

profile of v2, /device:TPU:34, one launch (start us, length us, event | category | flops | bytes accessed | tf_op | source)
XLA Modules:
  0.0 54.1 jit_solution(10930544964854254054)
XLA Ops:
  0.6 51.9 %shard_map.77 = (f32[16,32,128]{2,1,0:T(8,128)S(1)}, f32[2,16,128,128]{3,2,1,0:T(8,128)S(1)}) custom-call(f32[16,128,128]{2,1,0:T(8,128)} %courant_hbm.1, f32[1,2,16,128,128]{4,3,2,1,0:T(8,128)} %adjoint_hbm.1, bf16[1,6,16,128,128]{4,3,2,1,0:T(8,128)(2,1)} %forward_hbm.1, f32[4,1024]{1,0:T(4,128)} %bitcast.2, s32[3,1,1024]{2,1,0:T(1,128)} %bitcast.3, ...), custom_call_target="tpu_custom_call" | custom-call | tf_op jit(solution)/shard_map/pallas_call | solution.py:498
  52.5 1.4 %shard_map.78 = (f32[16,32,128]{2,1,0:T(8,128)}, f32[1,2,16,128,128]{4,3,2,1,0:T(8,128)}) custom-call(f32[16,32,128]{2,1,0:T(8,128)S(1)} %get-tuple-element.4.gradient_ref, f32[2,16,128,128]{3,2,1,0:T(8,128)S(1)} %get-tuple-element.5.final_ref), custom_call_target="tpu_custom_call" | custom-call | tf_op jit(solution)/shard_map/pallas_call | solution.py:555

commit v3 on v2

--- a/solution.py
+++ b/solution.py
@@ -11,7 +11,7 @@
 RADIUS = 6
 WIDTH = 4
 PAD = 8
-CHUNKS = 2
+CHUNKS = 4
 BLOCKS = 4
 MESH = pl.DeviceIdType.MESH
 
@@ -51,6 +51,7 @@
     along,
     band,
     spots,
+    across,
     amounts,
     image,
     taper_z,
@@ -100,6 +101,14 @@
             source, target = forward_hbm.at[0, :, z], forward.at[:, q]
         return pltpu.make_async_copy(source, target, in_sem.at[kind, q])
 
+    barrier = pltpu.get_barrier_semaphore()
+    for axis, target in (("dom", near), ("shot", shot_a), ("shot", shot_b)):
+        pl.semaphore_signal(barrier, inc=1, device_id={axis: target}, device_id_type=MESH)
+
+    @pl.when(has_far)
+    def _():
+        pl.semaphore_signal(barrier, inc=1, device_id={"dom": far}, device_id_type=MESH)
+
     tables = [
         pltpu.make_async_copy(source, target, table_sem.at[i])
         for i, (source, target) in enumerate(
@@ -113,14 +122,6 @@
         for q in order:
             load(kind, q).start()
 
-    barrier = pltpu.get_barrier_semaphore()
-    for axis, target in (("dom", near), ("shot", shot_a), ("shot", shot_b)):
-        pl.semaphore_signal(barrier, inc=1, device_id={axis: target}, device_id_type=MESH)
-
-    @pl.when(has_far)
-    def _():
-        pl.semaphore_signal(barrier, inc=1, device_id={"dom": far}, device_id_type=MESH)
-
     for level in (1, 2, 3, 4):
         for q in range(planes):
             zero = jnp.zeros((PAD, size_y), jnp.float32)
@@ -138,22 +139,19 @@
         weights = jnp.where(gap == k, OFFSET[k], weights)
     band[...] = weights.astype(jnp.bfloat16)
 
-    for table in tables:
+    for table in tables[:2]:
         table.wait()
 
     z_index = receivers_ref[0] - first_row
     z_index = z_index + parity * (planes - 1 - 2 * z_index)
-    cell_row = z_index * size_x + receivers_ref[1]
-    count = cell_row.shape[1]
+    count = z_index.shape[1]
 
     def spots_of():
-        def body(i, carry):
-            ids = lax.broadcasted_iota(jnp.int32, (16, count), 0) + i * 16
-            hit = jnp.where(ids == cell_row, 1.0, 0.0)
-            spots[pl.ds(pl.multiple_of(i * 16, 16), 16), :] = hit.astype(jnp.bfloat16)
-            return carry
-
-        lax.fori_loop(0, planes * size_x // 16, body, 0)
+        ids = lax.broadcasted_iota(jnp.int32, (size_x, count), 0)
+        across[...] = jnp.where(ids == receivers_ref[1], 1.0, 0.0).astype(jnp.bfloat16)
+        for q in range(planes):
+            level = jnp.where(z_index == q, 1.0, 0.0).astype(jnp.bfloat16)
+            spots[pl.ds(q * size_x, size_x), :] = across[...] * level
 
     def amounts_of(step):
         value = traces_ref[pl.ds(step, 1), :]
@@ -172,6 +170,7 @@
         lax.fori_loop(0, size_y // 16, body, 0)
 
     def tapers():
+        tables[2].wait()
         q_index = lax.broadcasted_iota(jnp.int32, (planes, size_y), 0)
         z_gap = q_index + parity * (planes - 1 - 2 * q_index) + first_row - source_ref[0, 0]
         taper_z[...] = jnp.exp((z_gap * z_gap).astype(jnp.float32) * (-1.0 / (RADIUS * RADIUS)))
@@ -181,9 +180,7 @@
         taper_xy[...] = jnp.exp(square.astype(jnp.float32) * (-1.0 / (RADIUS * RADIUS)))
 
     spots_of()
-    for step in range(ITERS):
-        amounts_of(step)
-    tapers()
+    amounts_of(3)
 
     @pl.when(has_far)
     def _():
@@ -231,12 +228,18 @@
         load(0, q).wait()
     near_copy(4).start()
 
-    def inject(step):
-        both = lax.dot_general(
-            spots[...], amounts[step], (((1,), (1,)), ((), ())), preferred_element_type=jnp.float32
-        )
-        added = both[:, :size_y] + both[:, size_y:]
-        lam[step][:, pl.ds(PAD, size_x), :] = added.reshape(planes, size_x, size_y)
+    def inject(step, first, last):
+        half = (last - first) * WIDTH // 2
+        for part in range(2):
+            start = first * WIDTH + part * half
+            both = lax.dot_general(
+                spots[pl.ds(start * size_x, half * size_x), :],
+                amounts[step],
+                (((1,), (1,)), ((), ())),
+                preferred_element_type=jnp.float32,
+            )
+            added = both[:, :size_y] + both[:, size_y:]
+            lam[step][pl.ds(start, half), pl.ds(PAD, size_x), :] = added.reshape(half, size_x, size_y)
 
     def lateral(level, first, last):
         here = pl.ds(first * WIDTH, (last - first) * WIDTH)
@@ -333,10 +336,9 @@
             device_id_type=MESH,
         )
 
-    def reduce_start(block):
+    def reduce_start(block, which):
         for side in range(2):
-            for which in (1, 0):
-                first_copy(block, side, which).start()
+            first_copy(block, side, which).start()
 
     def reduce_next(block):
         for side in range(2):
@@ -366,15 +368,19 @@
     def wait_near(level):
         near_copy(level).wait_recv()
 
-    def wave(step, first, second):
-        for c, fill in enumerate((first, second)):
-            far_wait(step + 1, c)
-            finish(step, c)
-            if step > 0:
-                far_start(step, c)
-            fill()
-
-    inject(3)
+    def take(step, c):
+        far_wait(step + 1, c)
+        finish(step, c)
+        if step > 0:
+            far_start(step, c)
+
+    def edge(step):
+        wait_near(step + 1)
+        advance(step, 3)
+        if step > 0:
+            near_copy(step).start()
+
+    inject(3, 0, 4)
     for q in range(WIDTH, planes - WIDTH):
         load(0, q).wait()
     for kind in (1, 2):
@@ -382,80 +388,74 @@
             load(kind, q).wait()
     lateral(4, 0, 4)
     advance(3, 0)
+    edge(3)
+    take(3, 0)
     advance(3, 2)
-    wait_near(4)
-    advance(3, 3)
-    near_copy(3).start()
+    amounts_of(2)
+    take(3, 1)
     advance(3, 1)
-
-    def first_3():
-        lateral(3, 1, 4)
-        inject(2)
-        advance(2, 2)
-        wait_near(3)
-        advance(2, 3)
-        near_copy(2).start()
-
-    def second_3():
-        lateral(3, 0, 1)
-        inject(1)
-        advance(2, 0)
-        lateral(2, 3, 4)
-        advance(2, 1)
-        wait_near(2)
-        advance(1, 3)
-        near_copy(1).start()
-
-    def first_2():
-        lateral(2, 1, 3)
-        inject(0)
-        advance(1, 2)
-        for q in order:
-            load(3, q).wait()
-
-    def second_2():
-        lateral(2, 0, 1)
-        lateral(1, 3, 4)
-        advance(1, 0)
-        advance(1, 1)
-        wait_near(1)
-        advance(0, 3)
-        imaging(3)
-        reduce_start(3)
-
-    def first_1():
-        lateral(1, 1, 3)
-        advance(0, 2)
-        imaging(2)
-        reduce_start(2)
-        reduce_next(3)
-
-    def second_1():
-        lateral(1, 0, 1)
-        advance(0, 1)
-        imaging(1)
-        reduce_start(1)
-        advance(0, 0)
-        reduce_next(2)
-        for block in range(1, BLOCKS):
-            store(0, block)
-
-    wave(3, first_3, second_3)
-    wave(2, first_2, second_2)
-    wave(1, first_1, second_1)
-    wave(0, lambda: None, lambda: None)
-    imaging(0)
-    reduce_start(0)
-    store(0, 0)
+    amounts_of(1)
+    take(3, 2)
+    inject(2, 0, 4)
+    take(3, 3)
+
+    lateral(3, 0, 4)
+    advance(2, 0)
+    take(2, 0)
+    edge(2)
+    advance(2, 2)
+    take(2, 1)
+    advance(2, 1)
+    amounts_of(0)
+    take(2, 2)
+    inject(1, 0, 4)
+    take(2, 3)
+
+    lateral(2, 0, 4)
+    advance(1, 0)
+    take(1, 0)
+    edge(1)
+    advance(1, 2)
+    take(1, 1)
+    inject(0, 2, 4)
+    lateral(1, 2, 4)
+    edge(0)
+    tapers()
+    for q in order:
+        load(3, q).wait()
+    imaging(3)
+    reduce_start(3, 1)
+    reduce_start(3, 0)
+    take(1, 2)
+    advance(1, 1)
+    inject(0, 0, 2)
+    take(1, 3)
+
+    lateral(1, 0, 2)
+    advance(0, 2)
+    imaging(2)
+    reduce_start(2, 1)
+    reduce_start(2, 0)
+    advance(0, 0)
+    take(0, 0)
+    advance(0, 1)
+    imaging(1)
+    reduce_start(1, 1)
+    take(0, 1)
     for block in range(BLOCKS):
         store(1, block)
-    reduce_end(3)
+    for block in range(1, BLOCKS):
+        store(0, block)
+    take(0, 2)
+    reduce_next(3)
+    take(0, 3)
+    imaging(0)
+    reduce_start(0, 1)
+    reduce_start(1, 0)
+    reduce_start(0, 0)
+    store(0, 0)
+    reduce_next(2)
     reduce_next(1)
-    reduce_end(2)
-    reduce_next(0)
-    reduce_end(1)
-    reduce_end(0)
-
     for level in (1, 2, 3, 4):
         near_copy(level).wait_send()
 
@@ -464,11 +464,17 @@
             for c in range(CHUNKS):
                 far_copy(level, c).wait_send()
 
+    reduce_next(0)
+    reduce_end(3)
+    reduce_end(2)
+    reduce_end(1)
     for block in range(BLOCKS):
         for side in range(2):
             first_copy(block, side, 0).wait_send()
             first_copy(block, side, 1).wait_send()
             second_copy(block, side).wait_send()
+    reduce_end(0)
+
 
 def write_out(gradient_ref, final_ref, gradient_hbm, final_hbm, sem):
     copies = [pltpu.make_async_copy(gradient_ref, gradient_hbm, sem.at[0])]
@@ -516,6 +522,7 @@
             pltpu.VMEM(grid3, f32),
             pltpu.VMEM((2 * size_y, size_y), bf16),
             pltpu.VMEM((planes * size_x, count), bf16),
+            pltpu.VMEM((size_x, count), bf16),
             pltpu.VMEM((ITERS, 2 * size_y, count), bf16),
             pltpu.VMEM(grid3, f32),
             pltpu.VMEM((planes, size_y), f32),

time: 54.2 us -> 47.9 us (0.88)
  the two profiles are of different devices: /device:TPU:34 before, /device:TPU:33 now
where the time goes in v3:
time: 47.9 us; the launch traced here: 47.8 us
  Pallas kernels  47.1 us (98%)
  between operations  0.64 us (1%)
    pallas_call x1, Pallas kernels, per_device(): pl.pallas_call(functools.partial(kernel, planes, size_x, size_y, dom_size...  45.7 us
    pallas_call x1, Pallas kernels, per_device(): pl.pallas_call(write_out, out_shape=(jax.ShapeDtypeStruct(gradient.shape,...  1.44 us

profile of v3, /device:TPU:33, one launch (start us, length us, event | category | flops | bytes accessed | tf_op | source)
XLA Modules:
  0.0 47.8 jit_solution(3009796490763174554)
XLA Ops:
  0.6 45.7 %shard_map.77 = (f32[16,32,128]{2,1,0:T(8,128)S(1)}, f32[2,16,128,128]{3,2,1,0:T(8,128)S(1)}) custom-call(f32[16,128,128]{2,1,0:T(8,128)} %courant_hbm.1, f32[1,2,16,128,128]{4,3,2,1,0:T(8,128)} %adjoint_hbm.1, bf16[1,6,16,128,128]{4,3,2,1,0:T(8,128)(2,1)} %forward_hbm.1, f32[4,1024]{1,0:T(4,128)} %bitcast.2, s32[3,1,1024]{2,1,0:T(1,128)} %bitcast.3, ...), custom_call_target="tpu_custom_call" | custom-call | tf_op jit(solution)/shard_map/pallas_call | solution.py:504
  46.3 1.4 %shard_map.78 = (f32[16,32,128]{2,1,0:T(8,128)}, f32[1,2,16,128,128]{4,3,2,1,0:T(8,128)}) custom-call(f32[16,32,128]{2,1,0:T(8,128)S(1)} %get-tuple-element.4.gradient_ref, f32[2,16,128,128]{3,2,1,0:T(8,128)S(1)} %get-tuple-element.5.final_ref), custom_call_target="tpu_custom_call" | custom-call | tf_op jit(solution)/shard_map/pallas_call | solution.py:562

commit v4 on v3

v4 whole, which is shorter than its diff:
```python
import functools

import jax
import jax.numpy as jnp
from jax import lax
from jax.experimental import pallas as pl
from jax.experimental.pallas import tpu as pltpu
from jax.sharding import PartitionSpec as P

ITERS = 4
RADIUS = 6
WIDTH = 4
PAD = 8
CHUNKS = 4
BLOCKS = 4
MESH = pl.DeviceIdType.MESH


def in_hbm(array):
    return pltpu.with_memory_space_constraint(array, pltpu.HBM)

SCALE = 5040.0
CENTRE = 3.0 * -14350.0
OFFSET = (0.0, 8064.0, -1008.0, 128.0, -9.0)


def make_band(band):
    size_y = band.shape[1]
    row = lax.broadcasted_iota(jnp.int32, (2 * size_y, size_y), 0) % size_y
    gap = jnp.abs(row - lax.broadcasted_iota(jnp.int32, (2 * size_y, size_y), 1))
    weights = jnp.zeros(gap.shape, jnp.float32)
    for k in range(1, WIDTH + 1):
        weights = jnp.where(gap == k, OFFSET[k], weights)
    band[...] = weights.astype(jnp.bfloat16)


def stencil(lam, base, later, courant, along, band, far_halo, near_halo):
    planes, size_x, size_y = courant.shape
    rows = size_x // CHUNKS
    zero_row = (lax.axis_index("dom") // lax.axis_size("dom")) * 8

    def lateral(level, first, last):
        for block in range(first, last):
            here = pl.ds(block * WIDTH, WIDTH)
            field = lam[level][here, pl.ds(PAD, size_x), :].reshape(-1, size_y)
            high = field.astype(jnp.bfloat16)
            low = (field - high.astype(jnp.float32)).astype(jnp.bfloat16)
            result = jnp.dot(
                jnp.concatenate([high, low], axis=1), band[...], preferred_element_type=jnp.float32
            )
            along[here, :, :] = result.reshape(WIDTH, size_x, size_y)

    def advance(step, block):
        now = lam[step + 1]
        before = later if step == 3 else lam[step + 2]
        offset = 0 if step == 3 else PAD
        low, high = block * WIDTH, (block + 1) * WIDTH
        for i in range(size_x // 8):
            at = zero_row + i * 8
            here = pl.ds(pl.multiple_of(at, 8), 8)
            padded = pl.ds(pl.multiple_of(at + PAD, 8), 8)
            column = {}
            for q in range(low - WIDTH, high + WIDTH):
                if 0 <= q < planes:
                    column[q] = now[q, padded, :]
                elif q >= planes:
                    column[q] = near_halo[step, WIDTH - 1 - (q - planes), here, :]
            for q in range(low, high):
                centre = column[q]
                total = along[q, here, :] + CENTRE * centre
                for k in range(1, WIDTH + 1):
                    beside = now[q, pl.ds(at + PAD + k, 8), :] + now[q, pl.ds(at + PAD - k, 8), :]
                    beside = beside + column[q + k]
                    if q - k >= 0:
                        beside = beside + column[q - k]
                    total = total + OFFSET[k] * beside
                moved = 2.0 * centre - before[q, pl.ds(pl.multiple_of(at + offset, 8), 8), :]
                scaled = courant[q, here, :] * (1.0 / SCALE)
                lam[step][q, padded, :] = base[step][q, padded, :] + (moved + scaled * total)

    def finish(step, c):
        for i in range(rows // 8):
            at = zero_row + c * rows + i * 8
            here = pl.ds(pl.multiple_of(at, 8), 8)
            padded = pl.ds(pl.multiple_of(at + PAD, 8), 8)
            beyond = [far_halo[step, d, here, :] for d in range(WIDTH)]
            for q in range(WIDTH):
                total = OFFSET[q + 1] * beyond[0]
                for d in range(1, WIDTH - q):
                    total = total + OFFSET[q + 1 + d] * beyond[d]
                scaled = courant[q, here, :] * (1.0 / SCALE)
                lam[step][q, padded, :] = lam[step][q, padded, :] + scaled * total

    return lateral, advance, finish


def backward(
    planes,
    size_x,
    size_y,
    dom_size,
    courant_hbm,
    adjoint_hbm,
    forward_hbm,
    traces_hbm,
    receivers_hbm,
    source_hbm,
    lam0,
    lam1,
    lam2,
    lam3,
    courant,
    forward,
    taper_z,
    taper_xy,
    far_last,
    near_last,
    traces_ref,
    receivers_ref,
    source_ref,
    lam4,
    later,
    along,
    band,
    spots,
    across,
    amounts,
    far_halo,
    near_halo,
    in_sem,
    table_sem,
    far_send,
    far_recv,
    near_send,
    near_recv,
):
    lam = (lam0, lam1, lam2, lam3, lam4)
    dom = lax.axis_index("dom")
    parity = dom % 2
    first_row = dom * planes
    far = dom + 2 * parity - 1
    near = dom + 1 - 2 * parity
    has_far = (far >= 0) & (far < dom_size)
    rows = size_x // CHUNKS

    def depth(q):
        return q + parity * (planes - 1 - 2 * q)

    def load(kind, q):
        z = depth(q)
        if kind == 0:
            source, target = adjoint_hbm.at[0, 1, z], lam4.at[q, pl.ds(PAD, size_x)]
        elif kind == 1:
            source, target = adjoint_hbm.at[0, 0, z], later.at[q]
        elif kind == 2:
            source, target = courant_hbm.at[z], courant.at[q]
        else:
            source, target = forward_hbm.at[0, :, z], forward.at[:, q]
        return pltpu.make_async_copy(source, target, in_sem.at[kind, q])

    barrier = pltpu.get_barrier_semaphore()
    pl.semaphore_signal(barrier, inc=1, device_id={"dom": near}, device_id_type=MESH)

    @pl.when(has_far)
    def _():
        pl.semaphore_signal(barrier, inc=1, device_id={"dom": far}, device_id_type=MESH)

    tables = [
        pltpu.make_async_copy(source, target, table_sem.at[i])
        for i, (source, target) in enumerate(
            ((receivers_hbm, receivers_ref), (traces_hbm, traces_ref), (source_hbm, source_ref))
        )
    ]
    for table in tables:
        table.start()
    order = [0, 1, 2, 3] + list(range(planes - 1, 3, -1))
    for q in order:
        load(0, q).start()

    for level in (1, 2, 3, 4):
        for q in range(planes):
            zero = jnp.zeros((PAD, size_y), jnp.float32)
            lam[level][q, pl.ds(0, PAD), :] = zero
            lam[level][q, pl.ds(PAD + size_x, PAD), :] = zero

    @pl.when(jnp.logical_not(has_far))
    def _():
        far_halo[...] = jnp.zeros(far_halo.shape, jnp.float32)

    make_band(band)

    @pl.when(has_far)
    def _():
        pl.semaphore_wait(barrier, 2)

    @pl.when(jnp.logical_not(has_far))
    def _():
        pl.semaphore_wait(barrier, 1)

    def far_copy(level, c):
        return pltpu.make_async_remote_copy(
            src_ref=lam[level].at[pl.ds(0, WIDTH), pl.ds(PAD + c * rows, rows)],
            dst_ref=far_halo.at[level - 1, :, pl.ds(c * rows, rows)],
            send_sem=far_send.at[level - 1, c],
            recv_sem=far_recv.at[level - 1, c],
            device_id={"dom": far},
            device_id_type=MESH,
        )

    def near_copy(level):
        return pltpu.make_async_remote_copy(
            src_ref=lam[level].at[pl.ds(planes - WIDTH, WIDTH), pl.ds(PAD, size_x)],
            dst_ref=near_halo.at[level - 1],
            send_sem=near_send.at[level - 1],
            recv_sem=near_recv.at[level - 1],
            device_id={"dom": near},
            device_id_type=MESH,
        )

    def far_start(level, c):
        @pl.when(has_far)
        def _():
            far_copy(level, c).start()

    def far_wait(level, c):
        @pl.when(has_far)
        def _():
            far_copy(level, c).wait_recv()

    for q in range(WIDTH):
        load(0, q).wait()
    for c in range(CHUNKS):
        far_start(4, c)
    for q in range(planes - WIDTH, planes):
        load(0, q).wait()
    near_copy(4).start()

    for table in tables[:2]:
        table.wait()
    for kind in (1, 2, 3):
        for q in order:
            load(kind, q).start()

    z_index = receivers_ref[0] - first_row
    z_index = z_index + parity * (planes - 1 - 2 * z_index)
    count = z_index.shape[1]

    def spots_of():
        ids = lax.broadcasted_iota(jnp.int32, (size_x, count), 0)
        across[...] = jnp.where(ids == receivers_ref[1], 1.0, 0.0).astype(jnp.bfloat16)
        for q in range(planes):
            level = jnp.where(z_index == q, 1.0, 0.0).astype(jnp.bfloat16)
            spots[pl.ds(q * size_x, size_x), :] = across[...] * level

    def amounts_of(step):
        value = traces_ref[pl.ds(step, 1), :]
        high = value.astype(jnp.bfloat16).astype(jnp.float32)
        low = value - high
        last = receivers_ref[2]

        def body(i, carry):
            ids = lax.broadcasted_iota(jnp.int32, (16, count), 0) + i * 16
            hit = ids == last
            start = pl.multiple_of(i * 16, 16)
            amounts[step, pl.ds(start, 16), :] = jnp.where(hit, high, 0.0).astype(jnp.bfloat16)
            amounts[step, pl.ds(size_y + start, 16), :] = jnp.where(hit, low, 0.0).astype(jnp.bfloat16)
            return carry

        lax.fori_loop(0, size_y // 16, body, 0)

    def tapers():
        tables[2].wait()
        q_index = lax.broadcasted_iota(jnp.int32, (planes, size_y), 0)
        z_gap = q_index + parity * (planes - 1 - 2 * q_index) + first_row - source_ref[0, 0]
        taper_z[...] = jnp.exp((z_gap * z_gap).astype(jnp.float32) * (-1.0 / (RADIUS * RADIUS)))
        x_gap = lax.broadcasted_iota(jnp.int32, (size_x, size_y), 0) - source_ref[0, 1]
        y_gap = lax.broadcasted_iota(jnp.int32, (size_x, size_y), 1) - source_ref[0, 2]
        square = x_gap * x_gap + y_gap * y_gap
        taper_xy[...] = jnp.exp(square.astype(jnp.float32) * (-1.0 / (RADIUS * RADIUS)))

    spots_of()
    amounts_of(3)


    def inject(step, first, last):
        half = (last - first) * WIDTH // 2
        for part in range(2):
            start = first * WIDTH + part * half
            both = lax.dot_general(
                spots[pl.ds(start * size_x, half * size_x), :],
                amounts[step],
                (((1,), (1,)), ((), ())),
                preferred_element_type=jnp.float32,
            )
            added = both[:, :size_y] + both[:, size_y:]
            lam[step][pl.ds(start, half), pl.ds(PAD, size_x), :] = added.reshape(half, size_x, size_y)

    def advance(step, block):
        now = lam[step + 1]
        before = later if step == 3 else lam[step + 2]
        offset = 0 if step == 3 else PAD
        low, high = block * WIDTH, (block + 1) * WIDTH
        for i in range(size_x // 8):
            at = zero_row + i * 8
            here = pl.ds(pl.multiple_of(at, 8), 8)
            padded = pl.ds(pl.multiple_of(at + PAD, 8), 8)
            column = {}
            for q in range(low - WIDTH, high + WIDTH):
                if 0 <= q < planes:
                    column[q] = now[q, padded, :]
                elif q >= planes:
                    column[q] = near_halo[step, WIDTH - 1 - (q - planes), here, :]
            for q in range(low, high):
                centre = column[q]
                total = along[q, here, :] + CENTRE * centre
                for k in range(1, WIDTH + 1):
                    beside = now[q, pl.ds(at + PAD + k, 8), :] + now[q, pl.ds(at + PAD - k, 8), :]
                    beside = beside + column[q + k]
                    if q - k >= 0:
                        beside = beside + column[q - k]
                    total = total + OFFSET[k] * beside
                moved = 2.0 * centre - before[q, pl.ds(pl.multiple_of(at + offset, 8), 8), :]
                scaled = courant[q, here, :] * (1.0 / SCALE)
                lam[step][q, padded, :] = lam[step][q, padded, :] + (moved + scaled * total)

    lateral, advance, finish = stencil(lam, lam, later, courant, along, band, far_halo, near_halo)

    def wait_near(level):
        near_copy(level).wait_recv()

    def take(step, c):
        far_wait(step + 1, c)
        finish(step, c)
        if step > 0:
            far_start(step, c)

    def edge(step):
        wait_near(step + 1)
        advance(step, 3)
        if step > 0:
            near_copy(step).start()

    inject(3, 0, 4)
    for q in range(WIDTH, planes - WIDTH):
        load(0, q).wait()
    for kind in (1, 2):
        for q in order:
            load(kind, q).wait()
    lateral(4, 0, 4)
    advance(3, 0)
    edge(3)
    take(3, 0)
    advance(3, 2)
    amounts_of(2)
    take(3, 1)
    advance(3, 1)
    amounts_of(1)
    take(3, 2)
    inject(2, 0, 4)
    take(3, 3)

    lateral(3, 0, 4)
    advance(2, 0)
    take(2, 0)
    edge(2)
    advance(2, 2)
    take(2, 1)
    advance(2, 1)
    amounts_of(0)
    take(2, 2)
    inject(1, 0, 4)
    take(2, 3)

    lateral(2, 0, 4)
    advance(1, 0)
    take(1, 0)
    edge(1)
    advance(1, 2)
    take(1, 1)
    inject(0, 0, 4)
    tapers()
    take(1, 2)
    advance(1, 1)
    take(1, 3)

    for q in order:
        load(3, q).wait()
    wait_near(1)
    near_last[0] = near_halo[0]
    for c in range(CHUNKS):
        far_wait(1, c)
    far_last[0] = far_halo[0]
    for level in (1, 2, 3, 4):
        near_copy(level).wait_send()

        @pl.when(has_far)
        def _():
            for c in range(CHUNKS):
                far_copy(level, c).wait_send()


def gradient_of(
    planes,
    size_x,
    size_y,
    base,
    lam1,
    lam2,
    lam3,
    courant,
    forward,
    taper_z,
    taper_xy,
    far_halo,
    near_halo,
    gradient_ref,
    final_ref,
    lam0,
    along,
    band,
    image,
    got_first,
    sent_second,
    got_second,
    first_send,
    first_recv,
    second_send,
    second_recv,
):
    lam = (lam0, lam1, lam2, lam3)
    shot = lax.axis_index("shot")
    parity = lax.axis_index("dom") % 2
    shot_a = shot + 1 - 2 * (shot % 2)
    shot_b = 3 - shot
    shot_c = (shot + 2) % 4

    def depth(q):
        return q + parity * (planes - 1 - 2 * q)

    barrier = pltpu.get_barrier_semaphore()
    for target in (shot_a, shot_b):
        pl.semaphore_signal(barrier, inc=1, device_id={"shot": target}, device_id_type=MESH)

    make_band(band)
    lateral, advance, finish = stencil(lam, (base,), None, courant, along, band, far_halo, near_halo)

    def imaging(block):
        def body(i, carry):
            at = pl.multiple_of(i * 16, 16)
            here = pl.ds(at, 16)
            padded = pl.ds(pl.multiple_of(at + PAD, 8), 16)
            across = taper_xy[here, :]
            for q in range(block * WIDTH, (block + 1) * WIDTH):
                saved = [forward[j, q, here, :].astype(jnp.float32) for j in range(ITERS + 2)]
                total = None
                for step in range(ITERS):
                    accel = saved[step + 2] - 2.0 * saved[step + 1] + saved[step]
                    term = lam[step][q, padded, :] * accel
                    total = term if total is None else total + term
                image[q, here, :] = total * (1.0 - taper_z[pl.ds(q, 1), :] * across)
            return carry

        lax.fori_loop(0, size_x // 16, body, 0)

    piece = size_x // 4

    def first_copy(block, side, which):
        q = block * WIDTH + 2 * side
        target = (shot_a, shot_b)[side]
        part = (target, shot_c)[which]
        return pltpu.make_async_remote_copy(
            src_ref=image.at[pl.ds(q, 2), pl.ds(pl.multiple_of(part * piece, 8), piece)],
            dst_ref=got_first.at[block, side, which],
            send_sem=first_send.at[block, side, which],
            recv_sem=first_recv.at[block, side, which],
            device_id={"shot": target},
            device_id_type=MESH,
        )

    def second_copy(block, side):
        return pltpu.make_async_remote_copy(
            src_ref=sent_second.at[block, side],
            dst_ref=got_second.at[block, side],
            send_sem=second_send.at[block, side],
            recv_sem=second_recv.at[block, side],
            device_id={"shot": (shot_b, shot_a)[side]},
            device_id_type=MESH,
        )

    def reduce_start(block, which):
        for side in range(2):
            first_copy(block, side, which).start()

    def reduce_next(block):
        for side in range(2):
            onward = (shot_b, shot_a)[side]
            q = block * WIDTH + 2 * side
            first_copy(block, side, 1).wait_recv()
            sent_second[block, side] = (
                image[pl.ds(q, 2), pl.ds(pl.multiple_of(onward * piece, 8), piece), :]
                + got_first[block, side, 1]
            )
            second_copy(block, side).start()

    def reduce_end(block):
        for side in range(2):
            first_copy(block, side, 0).wait_recv()
            second_copy(block, side).wait_recv()
            q = block * WIDTH + 2 * side
            own = image[pl.ds(q, 2), pl.ds(pl.multiple_of(shot * piece, 8), piece), :]
            own = own + got_first[block, side, 0] + got_second[block, side]
            for j in range(2):
                gradient_ref[depth(q + j)] = own[j]

    def store(level, block):
        for q in range(block * WIDTH, (block + 1) * WIDTH):
            final_ref[1 - level, depth(q)] = lam[level][q, pl.ds(PAD, size_x), :]

    lateral(1, 0, 4)
    advance(0, 3)
    imaging(3)
    pl.semaphore_wait(barrier, 2)
    reduce_start(3, 1)
    reduce_start(3, 0)
    advance(0, 2)
    imaging(2)
    reduce_start(2, 1)
    reduce_start(2, 0)
    advance(0, 1)
    imaging(1)
    reduce_start(1, 1)
    advance(0, 0)
    for c in range(CHUNKS):
        finish(0, c)
    imaging(0)
    reduce_start(0, 1)
    reduce_start(1, 0)
    reduce_start(0, 0)
    for level in range(2):
        for block in range(BLOCKS):
            store(level, block)
    reduce_next(3)
    reduce_next(2)
    reduce_next(1)
    reduce_next(0)
    reduce_end(3)
    reduce_end(2)
    reduce_end(1)
    for block in range(BLOCKS):
        for side in range(2):
            first_copy(block, side, 0).wait_send()
            first_copy(block, side, 1).wait_send()
            second_copy(block, side).wait_send()
    reduce_end(0)


def write_out(gradient_ref, final_ref, gradient_hbm, final_hbm, sem):
    copies = [pltpu.make_async_copy(gradient_ref, gradient_hbm, sem.at[0])]
    half = final_ref.shape[1] // 2
    for level in range(2):
        for part in range(2):
            at = pl.ds(part * half, half)
            copies.append(
                pltpu.make_async_copy(
                    final_ref.at[level, at], final_hbm.at[0, level, at], sem.at[1 + 2 * level + part]
                )
            )
    for copy in copies:
        copy.start()
    for copy in copies:
        copy.wait()


def per_device(dom_size, courant_sq, adjoint_init, forward_saved, residual_traces, receivers, sources):
    planes, size_x, size_y = courant_sq.shape
    count = receivers.shape[1]
    f32, bf16 = jnp.float32, jnp.bfloat16
    padded = pltpu.VMEM((planes, size_x + 2 * PAD, size_y), f32)
    grid3 = (planes, size_x, size_y)
    dma = pltpu.SemaphoreType.DMA
    piece = (2, size_x // 4, size_y)
    hbm = pl.BlockSpec(memory_space=pltpu.HBM)
    vmem = pl.BlockSpec(memory_space=pltpu.VMEM)
    padded_shape = (planes, size_x + 2 * PAD, size_y)
    halo = (1, WIDTH, size_x, size_y)
    arrays = (
        courant_sq,
        adjoint_init,
        forward_saved,
        residual_traces[0],
        receivers.transpose(2, 0, 1),
        sources,
    )
    done = pl.pallas_call(
        functools.partial(backward, planes, size_x, size_y, dom_size),
        out_shape=tuple(jax.ShapeDtypeStruct(padded_shape, f32) for _ in range(4))
        + (
            jax.ShapeDtypeStruct(grid3, f32),
            jax.ShapeDtypeStruct((ITERS + 2,) + grid3, bf16),
            jax.ShapeDtypeStruct((planes, size_y), f32),
            jax.ShapeDtypeStruct((size_x, size_y), f32),
            jax.ShapeDtypeStruct(halo, f32),
            jax.ShapeDtypeStruct(halo, f32),
        ),
        in_specs=[hbm] * 6,
        out_specs=(vmem,) * 10,
        scratch_shapes=[
            pltpu.VMEM((ITERS, count), f32),
            pltpu.VMEM((3, 1, count), jnp.int32),
            pltpu.SMEM((1, 3), jnp.int32),
            padded,
            pltpu.VMEM(grid3, f32),
            pltpu.VMEM(grid3, f32),
            pltpu.VMEM((2 * size_y, size_y), bf16),
            pltpu.VMEM((planes * size_x, count), bf16),
            pltpu.VMEM((size_x, count), bf16),
            pltpu.VMEM((ITERS, 2 * size_y, count), bf16),
            pltpu.VMEM((ITERS, WIDTH, size_x, size_y), f32),
            pltpu.VMEM((ITERS, WIDTH, size_x, size_y), f32),
            dma((4, planes)),
            dma((3,)),
            dma((ITERS, CHUNKS)),
            dma((ITERS, CHUNKS)),
            dma((ITERS,)),
            dma((ITERS,)),
        ],
        compiler_params=pltpu.CompilerParams(
            collective_id=0, has_side_effects=True, vmem_limit_bytes=28 * 1024 * 1024
        ),
    )(*(in_hbm(array) for array in arrays))
    gradient, final = pl.pallas_call(
        functools.partial(gradient_of, planes, size_x, size_y),
        out_shape=(
            jax.ShapeDtypeStruct((planes, size_x // 4, size_y), f32),
            jax.ShapeDtypeStruct((2, planes, size_x, size_y), f32),
        ),
        in_specs=[vmem] * 10,
        out_specs=(vmem, vmem),
        scratch_shapes=[
            padded,
            pltpu.VMEM(grid3, f32),
            pltpu.VMEM((2 * size_y, size_y), bf16),
            pltpu.VMEM(grid3, f32),
            pltpu.VMEM((BLOCKS, 2, 2) + piece, f32),
            pltpu.VMEM((BLOCKS, 2) + piece, f32),
            pltpu.VMEM((BLOCKS, 2) + piece, f32),
            dma((BLOCKS, 2, 2)),
            dma((BLOCKS, 2, 2)),
            dma((BLOCKS, 2)),
            dma((BLOCKS, 2)),
        ],
        compiler_params=pltpu.CompilerParams(
            collective_id=1, has_side_effects=True, vmem_limit_bytes=20 * 1024 * 1024
        ),
    )(*done)
    return pl.pallas_call(
        write_out,
        out_shape=(
            jax.ShapeDtypeStruct(gradient.shape, f32),
            jax.ShapeDtypeStruct((1,) + final.shape, f32),
        ),
        in_specs=[pl.BlockSpec(memory_space=pltpu.VMEM)] * 2,
        out_specs=(pl.BlockSpec(memory_space=pl.ANY),) * 2,
        scratch_shapes=[dma((5,))],
        compiler_params=pltpu.CompilerParams(vmem_limit_bytes=8 * 1024 * 1024),
    )(gradient, final)


def solution(mesh):
    placed = (
        P(("groups", "dom"), None, None),
        P(("groups", "shot"), None, "dom", None, None),
        P(("groups", "shot"), None, "dom", None, None),
        P(("groups", "shot"), None, None),
        P(("groups", "shot"), None, None),
        P(("groups", "shot"), None),
    )
    return jax.shard_map(
        functools.partial(per_device, mesh.shape["dom"]),
        mesh=mesh,
        in_specs=placed,
        out_specs=(
            P(("groups", "dom"), "shot", None),
            P(("groups", "shot"), None, "dom", None, None),
        ),
        check_vma=False,
    )
```

time: 47.9 us -> 49.7 us (1.038)
  Pallas kernels: 47.1 us -> 48.7 us
    pallas_call x1 -> x2, Pallas kernels: 45.7 us -> 47.3 us  [the longest x1 36.5 us: per_device(): pl.pallas_call(functools.partial(backward, planes, size_x, size_y, dom_si...]
where the time goes in v4:
time: 49.7 us; the launch traced here: 49.5 us
  Pallas kernels  48.7 us (98%)
  between operations  0.81 us (2%)
    pallas_call x1, Pallas kernels, per_device(): pl.pallas_call(functools.partial(backward, planes, size_x, size_y, dom_si...  36.5 us
    pallas_call x1, Pallas kernels, per_device(): pl.pallas_call(functools.partial(gradient_of, planes, size_x, size_y), ou...  10.8 us
    pallas_call x1, Pallas kernels, per_device(): pl.pallas_call(write_out, out_shape=(jax.ShapeDtypeStruct(gradient.shape,...  1.44 us

profile of v4, /device:TPU:33, one launch (start us, length us, event | category | flops | bytes accessed | tf_op | source)
XLA Modules:
  0.0 49.5 jit_solution(14552430659001522630)
XLA Ops:
  0.6 36.5 %shard_map.77 = (f32[16,144,128]{2,1,0:T(8,128)S(1)}, f32[16,144,128]{2,1,0:T(8,128)S(1)}, f32[16,144,128]{2,1,0:T(8,128)S(1)}, f32[16,144,128]{2,1,0:T(8,128)S(...) custom-call(f32[16,128,128]{2,1,0:T(8,128)} %courant_hbm.1, ...), custom_call_target="tpu_custom_call" | custom-call | tf_op jit(solution)/shard_map/pallas_call | solution.py:594
  37.2 10.8 %shard_map.78 = (f32[16,32,128]{2,1,0:T(8,128)S(1)}, f32[2,16,128,128]{3,2,1,0:T(8,128)S(1)}) custom-call(f32[16,144,128]{2,1,0:T(8,128)S(1)} %get-tuple-element.14.base, f32[16,144,128]{2,1,0:T(8,128)S(1)} %get-tuple-element.15.lam1, f32[16,144,128]{2,1,0:T(8,128)S(1)} %get-tuple-element.16.lam2, f32[16,144,128]{2,1,0:T(8,128)S(1)} %get-tuple-element.17.lam3, ...), custom_call_target="tpu_custom_call" | custom-call | tf_op jit(solution)/shard_map/pallas_call | solution.py:631
  47.9 1.4 %shard_map.79 = (f32[16,32,128]{2,1,0:T(8,128)}, f32[1,2,16,128,128]{4,3,2,1,0:T(8,128)}) custom-call(f32[16,32,128]{2,1,0:T(8,128)S(1)} %get-tuple-element.24.gradient_ref, f32[2,16,128,128]{3,2,1,0:T(8,128)S(1)} %get-tuple-element.25.final_ref), custom_call_target="tpu_custom_call" | custom-call | tf_op jit(solution)/shard_map/pallas_call | solution.py:656

commit v5 on v3

--- a/solution.py
+++ b/solution.py
@@ -118,9 +118,8 @@
     for table in tables:
         table.start()
     order = [0, 1, 2, 3] + list(range(planes - 1, 3, -1))
-    for kind in range(4):
-        for q in order:
-            load(kind, q).start()
+    for q in order:
+        load(0, q).start()
 
     for level in (1, 2, 3, 4):
         for q in range(planes):
@@ -139,8 +138,42 @@
         weights = jnp.where(gap == k, OFFSET[k], weights)
     band[...] = weights.astype(jnp.bfloat16)
 
+    def far_copy(level, c):
+        return pltpu.make_async_remote_copy(
+            src_ref=lam[level].at[pl.ds(0, WIDTH), pl.ds(PAD + c * rows, rows)],
+            dst_ref=far_halo.at[level - 1, :, pl.ds(c * rows, rows)],
+            send_sem=far_send.at[level - 1, c],
+            recv_sem=far_recv.at[level - 1, c],
+            device_id={"dom": far},
+            device_id_type=MESH,
+        )
+
+    def near_copy(level):
+        return pltpu.make_async_remote_copy(
+            src_ref=lam[level].at[pl.ds(planes - WIDTH, WIDTH), pl.ds(PAD, size_x)],
+            dst_ref=near_halo.at[level - 1],
+            send_sem=near_send.at[level - 1],
+            recv_sem=near_recv.at[level - 1],
+            device_id={"dom": near},
+            device_id_type=MESH,
+        )
+
+    def far_start(level, c):
+        @pl.when(has_far)
+        def _():
+            far_copy(level, c).start()
+
+    def far_wait(level, c):
+        @pl.when(has_far)
+        def _():
+            far_copy(level, c).wait_recv()
+
+
     for table in tables[:2]:
         table.wait()
+    for kind in (1, 2, 3):
+        for q in order:
+            load(kind, q).start()
 
     z_index = receivers_ref[0] - first_row
     z_index = z_index + parity * (planes - 1 - 2 * z_index)
@@ -182,51 +215,6 @@
     spots_of()
     amounts_of(3)
 
-    @pl.when(has_far)
-    def _():
-        pl.semaphore_wait(barrier, 4)
-
-    @pl.when(jnp.logical_not(has_far))
-    def _():
-        pl.semaphore_wait(barrier, 3)
-
-    def far_copy(level, c):
-        return pltpu.make_async_remote_copy(
-            src_ref=lam[level].at[pl.ds(0, WIDTH), pl.ds(PAD + c * rows, rows)],
-            dst_ref=far_halo.at[level - 1, :, pl.ds(c * rows, rows)],
-            send_sem=far_send.at[level - 1, c],
-            recv_sem=far_recv.at[level - 1, c],
-            device_id={"dom": far},
-            device_id_type=MESH,
-        )
-
-    def near_copy(level):
-        return pltpu.make_async_remote_copy(
-            src_ref=lam[level].at[pl.ds(planes - WIDTH, WIDTH), pl.ds(PAD, size_x)],
-            dst_ref=near_halo.at[level - 1],
-            send_sem=near_send.at[level - 1],
-            recv_sem=near_recv.at[level - 1],
-            device_id={"dom": near},
-            device_id_type=MESH,
-        )
-
-    def far_start(level, c):
-        @pl.when(has_far)
-        def _():
-            far_copy(level, c).start()
-
-    def far_wait(level, c):
-        @pl.when(has_far)
-        def _():
-            far_copy(level, c).wait_recv()
-
-    for q in range(WIDTH):
-        load(0, q).wait()
-    for c in range(CHUNKS):
-        far_start(4, c)
-    for q in range(planes - WIDTH, planes):
-        load(0, q).wait()
-    near_copy(4).start()
 
     def inject(step, first, last):
         half = (last - first) * WIDTH // 2
@@ -242,15 +230,15 @@
             lam[step][pl.ds(start, half), pl.ds(PAD, size_x), :] = added.reshape(half, size_x, size_y)
 
     def lateral(level, first, last):
-        here = pl.ds(first * WIDTH, (last - first) * WIDTH)
-        shape = ((last - first) * WIDTH, size_x, size_y)
-        field = lam[level][here, pl.ds(PAD, size_x), :].reshape(-1, size_y)
-        high = field.astype(jnp.bfloat16)
-        low = (field - high.astype(jnp.float32)).astype(jnp.bfloat16)
-        result = jnp.dot(
-            jnp.concatenate([high, low], axis=1), band[...], preferred_element_type=jnp.float32
-        )
-        along[here, :, :] = result.reshape(shape)
+        for block in range(first, last):
+            here = pl.ds(block * WIDTH, WIDTH)
+            field = lam[level][here, pl.ds(PAD, size_x), :].reshape(-1, size_y)
+            high = field.astype(jnp.bfloat16)
+            low = (field - high.astype(jnp.float32)).astype(jnp.bfloat16)
+            result = jnp.dot(
+                jnp.concatenate([high, low], axis=1), band[...], preferred_element_type=jnp.float32
+            )
+            along[here, :, :] = result.reshape(WIDTH, size_x, size_y)
 
     def advance(step, block):
         now = lam[step + 1]
@@ -380,44 +368,59 @@
         if step > 0:
             near_copy(step).start()
 
+    amounts_of(2)
+    amounts_of(1)
+    amounts_of(0)
     inject(3, 0, 4)
-    for q in range(WIDTH, planes - WIDTH):
+    for q in order:
         load(0, q).wait()
     for kind in (1, 2):
         for q in order:
             load(kind, q).wait()
     lateral(4, 0, 4)
     advance(3, 0)
+    advance(3, 2)
+    advance(3, 1)
+    inject(2, 0, 4)
+
+    @pl.when(has_far)
+    def _():
+        pl.semaphore_wait(barrier, 4)
+
+    @pl.when(jnp.logical_not(has_far))
+    def _():
+        pl.semaphore_wait(barrier, 3)
+
+    for c in range(CHUNKS):
+        far_start(4, c)
+    near_copy(4).start()
+    inject(1, 0, 4)
+    for c in range(CHUNKS):
+        take(3, c)
+
+    lateral(3, 0, 3)
+    advance(2, 0)
+    advance(2, 1)
     edge(3)
-    take(3, 0)
-    advance(3, 2)
-    amounts_of(2)
-    take(3, 1)
-    advance(3, 1)
-    amounts_of(1)
-    take(3, 2)
-    inject(2, 0, 4)
-    take(3, 3)
-
-    lateral(3, 0, 4)
-    advance(2, 0)
     take(2, 0)
-    edge(2)
+    lateral(3, 3, 4)
     advance(2, 2)
     take(2, 1)
-    advance(2, 1)
-    amounts_of(0)
+    edge(2)
     take(2, 2)
-    inject(1, 0, 4)
     take(2, 3)
 
     lateral(2, 0, 4)
     advance(1, 0)
     take(1, 0)
+    advance(1, 1)
+    take(1, 1)
+    advance(1, 2)
+    inject(0, 2, 4)
     edge(1)
-    advance(1, 2)
-    take(1, 1)
-    inject(0, 2, 4)
+    take(1, 2)
+    take(1, 3)
+
     lateral(1, 2, 4)
     edge(0)
     tapers()
@@ -426,11 +429,7 @@
     imaging(3)
     reduce_start(3, 1)
     reduce_start(3, 0)
-    take(1, 2)
-    advance(1, 1)
     inject(0, 0, 2)
-    take(1, 3)
-
     lateral(1, 0, 2)
     advance(0, 2)
     imaging(2)

time: 47.9 us -> 46.9 us (0.979)
  Pallas kernels: 47.1 us -> 45.6 us
    pallas_call x1, Pallas kernels: 45.7 us -> 44.2 us  [per_device(): pl.pallas_call(functools.partial(kernel, planes, size_x, size_y, dom_size...]
where the time goes in v5:
time: 46.9 us; the launch traced here: 46.4 us
  Pallas kernels  45.6 us (97%)
  between operations  0.8 us (2%)
    pallas_call x1, Pallas kernels, per_device(): pl.pallas_call(functools.partial(kernel, planes, size_x, size_y, dom_size...  44.2 us
    pallas_call x1, Pallas kernels, per_device(): pl.pallas_call(write_out, out_shape=(jax.ShapeDtypeStruct(gradient.shape,...  1.44 us

profile of v5, /device:TPU:33, one launch (start us, length us, event | category | flops | bytes accessed | tf_op | source)
XLA Modules:
  0.0 46.4 jit_solution(15141609641590863171)
XLA Ops:
  0.6 44.2 %shard_map.77 = (f32[16,32,128]{2,1,0:T(8,128)S(1)}, f32[2,16,128,128]{3,2,1,0:T(8,128)S(1)}) custom-call(f32[16,128,128]{2,1,0:T(8,128)} %courant_hbm.1, f32[1,2,16,128,128]{4,3,2,1,0:T(8,128)} %adjoint_hbm.1, bf16[1,6,16,128,128]{4,3,2,1,0:T(8,128)(2,1)} %forward_hbm.1, f32[4,1024]{1,0:T(4,128)} %bitcast.2, s32[3,1,1024]{2,1,0:T(1,128)} %bitcast.3, ...), custom_call_target="tpu_custom_call" | custom-call | tf_op jit(solution)/shard_map/pallas_call | solution.py:503
  44.8 1.4 %shard_map.78 = (f32[16,32,128]{2,1,0:T(8,128)}, f32[1,2,16,128,128]{4,3,2,1,0:T(8,128)}) custom-call(f32[16,32,128]{2,1,0:T(8,128)S(1)} %get-tuple-element.4.gradient_ref, f32[2,16,128,128]{3,2,1,0:T(8,128)S(1)} %get-tuple-element.5.final_ref), custom_call_target="tpu_custom_call" | custom-call | tf_op jit(solution)/shard_map/pallas_call | solution.py:561

commit v6 on v5

--- a/solution.py
+++ b/solution.py
@@ -416,8 +416,8 @@
     advance(1, 1)
     take(1, 1)
     advance(1, 2)
-    inject(0, 2, 4)
     edge(1)
+    inject(0, 0, 4)
     take(1, 2)
     take(1, 3)
 
@@ -429,7 +429,6 @@
     imaging(3)
     reduce_start(3, 1)
     reduce_start(3, 0)
-    inject(0, 0, 2)
     lateral(1, 0, 2)
     advance(0, 2)
     imaging(2)
@@ -446,13 +445,13 @@
     for block in range(1, BLOCKS):
         store(0, block)
     take(0, 2)
-    reduce_next(3)
     take(0, 3)
     imaging(0)
     reduce_start(0, 1)
     reduce_start(1, 0)
     reduce_start(0, 0)
     store(0, 0)
+    reduce_next(3)
     reduce_next(2)
     reduce_next(1)
     for level in (1, 2, 3, 4):

time: 46.9 us -> 46.9 us (level)
  no operation moved by 1% of the time
where the time goes in v6:
time: 46.9 us; the launch traced here: 46.7 us
  Pallas kernels  45.9 us (98%)
  between operations  0.8 us (2%)
    pallas_call x1, Pallas kernels, per_device(): pl.pallas_call(functools.partial(kernel, planes, size_x, size_y, dom_size...  44.5 us
    pallas_call x1, Pallas kernels, per_device(): pl.pallas_call(write_out, out_shape=(jax.ShapeDtypeStruct(gradient.shape,...  1.44 us

profile of v6, /device:TPU:33, one launch (start us, length us, event | category | flops | bytes accessed | tf_op | source)
XLA Modules:
  0.0 46.7 jit_solution(10235213176703021632)
XLA Ops:
  0.6 44.5 %shard_map.77 = (f32[16,32,128]{2,1,0:T(8,128)S(1)}, f32[2,16,128,128]{3,2,1,0:T(8,128)S(1)}) custom-call(f32[16,128,128]{2,1,0:T(8,128)} %courant_hbm.1, f32[1,2,16,128,128]{4,3,2,1,0:T(8,128)} %adjoint_hbm.1, bf16[1,6,16,128,128]{4,3,2,1,0:T(8,128)(2,1)} %forward_hbm.1, f32[4,1024]{1,0:T(4,128)} %bitcast.2, s32[3,1,1024]{2,1,0:T(1,128)} %bitcast.3, ...), custom_call_target="tpu_custom_call" | custom-call | tf_op jit(solution)/shard_map/pallas_call | solution.py:502
  45.1 1.4 %shard_map.78 = (f32[16,32,128]{2,1,0:T(8,128)}, f32[1,2,16,128,128]{4,3,2,1,0:T(8,128)}) custom-call(f32[16,32,128]{2,1,0:T(8,128)S(1)} %get-tuple-element.4.gradient_ref, f32[2,16,128,128]{3,2,1,0:T(8,128)S(1)} %get-tuple-element.5.final_ref), custom_call_target="tpu_custom_call" | custom-call | tf_op jit(solution)/shard_map/pallas_call | solution.py:560
